TPU v7x, 32 devices: a whole 2x2x4 slice. The times are simulated.
32 devices in a mesh: dp: 16 (over z, x, core), mp: 2 (over y).
Axes of the slice: x: 2, y: 2, z: 4, core: 2. Of those that a mesh axis runs over, the one named last changes fastest.
Arguments:
- patches: bfloat16 [12544, 768], P(('dp', 'mp')), may hold values from -6 to 6
- captions: bfloat16 [4096, 768], P(('dp', 'mp')), may hold values from -6 to 6
- patch_image: int32 [12544], P('dp'), may hold values from 0 to 3, as said below
- caption_image: int32 [32], P('dp'), may hold values from 0 to 3, as said below
- image_norm: float32 [768], replicated, may hold values from 0.5 to 1.5
- image_ffnorm: float32 [768], replicated, may hold values from 0.5 to 1.5
- text_norm: float32 [768], replicated, may hold values from 0.5 to 1.5
- cross_norm: float32 [768], replicated, may hold values from 0.5 to 1.5
- text_ffnorm: float32 [768], replicated, may hold values from 0.5 to 1.5
- image_proj: bfloat16 [768, 2304], P(None, 'mp'), may hold values from -0.21875 to 0.21875
- image_mix: bfloat16 [768, 768], P('mp'), may hold values from -1.25 to 1.25
- image_up: bfloat16 [768, 3072], P(None, 'mp'), may hold values from -0.21875 to 0.21875
- image_down: bfloat16 [3072, 768], P('mp'), may hold values from -0.109375 to 0.109375
- text_proj: bfloat16 [768, 2304], P(None, 'mp'), may hold values from -0.21875 to 0.21875
- text_mix: bfloat16 [768, 768], P('mp'), may hold values from -1.25 to 1.25
- cross_query: bfloat16 [768, 768], P(None, 'mp'), may hold values from -0.21875 to 0.21875
- cross_keyval: bfloat16 [768, 1536], P(None, 'mp'), may hold values from -0.21875 to 0.21875
- cross_mix: bfloat16 [768, 768], P('mp'), may hold values from -1.25 to 1.25
- text_up: bfloat16 [768, 3072], P(None, 'mp'), may hold values from -0.21875 to 0.21875
- text_down: bfloat16 [3072, 768], P('mp'), may hold values from -0.109375 to 0.109375
- image_cotan: bfloat16 [12544, 768], P(('dp', 'mp')), may hold values from -6 to 6
- text_cotan: bfloat16 [4096, 768], P(('dp', 'mp')), may hold values from -6 to 6
Outputs:
- image_embed: bfloat16 [12544, 768], P(('dp', 'mp'))
- text_embed: bfloat16 [4096, 768], P(('dp', 'mp'))
- grad_patches: bfloat16 [12544, 768], P(('dp', 'mp'))
- grad_captions: bfloat16 [4096, 768], P(('dp', 'mp'))
- grad_image_norm: float32 [768], replicated
- grad_image_ffnorm: float32 [768], replicated
- grad_text_norm: float32 [768], replicated
- grad_cross_norm: float32 [768], replicated
- grad_text_ffnorm: float32 [768], replicated
- grad_image_proj: float32 [768, 2304], P(None, 'mp')
- grad_image_mix: float32 [768, 768], P('mp')
- grad_image_up: float32 [768, 3072], P(None, 'mp')
- grad_image_down: float32 [3072, 768], P('mp')
- grad_text_proj: float32 [768, 2304], P(None, 'mp')
- grad_text_mix: float32 [768, 768], P('mp')
- grad_cross_query: float32 [768, 768], P(None, 'mp')
- grad_cross_keyval: float32 [768, 1536], P(None, 'mp')
- grad_cross_mix: float32 [768, 768], P('mp')
- grad_text_up: float32 [768, 3072], P(None, 'mp')
- grad_text_down: float32 [3072, 768], P('mp')
Inputs may be any that keep to these rules, and one draw needn't show every extreme that they name: `patch_image`: the 784 rows of a group form 1 aligned blocks of 784 rows; each block holds one image of 784 patches or four images of 196 patches in a row; images are numbered from 0 up in row order within the group. `caption_image`: each caption names an image of its own group.
All inputs are finite; a program needn't handle non-finite values.
Results may differ from a plain program's by a relative error of at most 0.024.
Values may be sent and summed in bfloat16 or wider, within the bound.
A program may use at most 192 MiB of HBM per device.

v0:
```python
import jax
import jax.numpy as jnp
from jax import lax
from jax.sharding import PartitionSpec as P

HD = 64
LT = 128


NEG_FILL = -1000000000.0
EPS = 1e-06


def norm_rows(values, gain_vec):
    row_mean = jnp.mean(values, axis=-1, keepdims=True)
    centred = values - row_mean
    row_var = jnp.mean(centred * centred, axis=-1, keepdims=True)
    inv_std = lax.rsqrt(row_var + EPS)
    scaled = centred * inv_std
    return (scaled * gain_vec, scaled, inv_std)


def norm_back(grad_out, scaled, inv_std, gain_vec):
    grad_scaled = grad_out * gain_vec
    grad_gain = jnp.sum(grad_out * scaled, axis=0)
    mean_grad = jnp.mean(grad_scaled, axis=-1, keepdims=True)
    mean_cross = jnp.mean(grad_scaled * scaled, axis=-1, keepdims=True)
    return (inv_std * (grad_scaled - mean_grad - scaled * mean_cross), grad_gain)


def gelu_exact(values):
    return jax.nn.gelu(values, approximate=False)


def product(form, left, right):
    return jnp.einsum(form, left, right, preferred_element_type=jnp.float32)


def heads_first(values):
    return jnp.swapaxes(values, 0, 1)


def attend_forward(queries, key_rows, value_rows, allowed):
    factor = queries.shape[-1] ** (-0.5)

    def per_head(pieces):
        query_head, key_head, value_head = pieces
        scores = product("qe,ke->qk", query_head, key_head) * factor
        scores = jnp.where(allowed, scores, NEG_FILL)
        row_max = jnp.max(scores, axis=-1, keepdims=True)
        exponent = jnp.exp(scores - row_max)
        totals = jnp.sum(exponent, axis=-1, keepdims=True)
        probability = (exponent / totals).astype(jnp.bfloat16)
        result = jnp.dot(probability, value_head, preferred_element_type=jnp.float32)
        return (result, (row_max + jnp.log(totals))[:, 0])

    result, log_sum = lax.map(
        per_head, (heads_first(queries), heads_first(key_rows), heads_first(value_rows))
    )
    return (heads_first(result), log_sum)


def attend_back(queries, key_rows, value_rows, allowed, log_sum, grad_att):
    factor = queries.shape[-1] ** (-0.5)

    def per_head(pieces):
        query_head, key_head, value_head, head_lse, grad_head = pieces
        scores = product("qe,ke->qk", query_head, key_head) * factor
        scores = jnp.where(allowed, scores, NEG_FILL)
        probability = jnp.exp(scores - head_lse[:, None])
        grad_value = product("qk,qe->ke", probability.astype(jnp.bfloat16), grad_head)
        grad_prob = product("qe,ke->qk", grad_head, value_head)
        row_dot = jnp.sum(probability * grad_prob, axis=-1, keepdims=True)
        grad_scores = (probability * (grad_prob - row_dot)).astype(jnp.bfloat16)
        grad_query = jnp.dot(grad_scores, key_head, preferred_element_type=jnp.float32) * factor
        grad_key = product("qk,qe->ke", grad_scores, query_head) * factor
        return (grad_query, grad_key, grad_value)

    grad_list = lax.map(
        per_head,
        (
            heads_first(queries),
            heads_first(key_rows),
            heads_first(value_rows),
            log_sum,
            heads_first(grad_att),
        ),
    )
    return tuple((heads_first(grad_piece) for grad_piece in grad_list))


def local(
    patches,
    captions,
    patch_image,
    caption_image,
    image_norm,
    image_ffnorm,
    text_norm,
    cross_norm,
    text_ffnorm,
    image_proj,
    image_mix,
    image_up,
    image_down,
    text_proj,
    text_mix,
    cross_query,
    cross_keyval,
    cross_mix,
    text_up,
    text_down,
    image_cotan,
    text_cotan,
):

    def spread(own_rows):
        return lax.all_gather(own_rows, "mp", axis=0, tiled=True)

    def collect(partial_rows):
        return lax.psum_scatter(partial_rows, "mp", scatter_dimension=0, tiled=True)

    def spread_grad(own_rows):
        return lax.all_gather(own_rows, "mp", axis=0, tiled=True)

    def collect_grad(partial_rows):
        return lax.psum_scatter(partial_rows, "mp", scatter_dimension=0, tiled=True)

    def normed_rows(own_rows):
        return lax.all_gather(own_rows, "mp", axis=0, tiled=True)

    group_rows = patch_image.shape[0]
    local_heads = image_proj.shape[1] // (3 * HD)
    same_image = patch_image[:, None] == patch_image[None, :]
    caption_count = caption_image.shape[0]
    text_rows = caption_count * LT
    position = jnp.arange(text_rows)
    caption_index = position // LT
    causal = (caption_index[:, None] == caption_index[None, :]) & (
        position[None, :] <= position[:, None]
    )
    row_image = jnp.broadcast_to(caption_image[:, None], (caption_count, LT)).reshape(text_rows)
    cross_allowed = row_image[:, None] == patch_image[None, :]

    def feed_back(grad_resid, whole_in, pre_act, hidden_act, weight_up, weight_down):
        grad_whole = spread_grad(grad_resid.astype(jnp.bfloat16))
        grad_down = product("rf,rd->fd", hidden_act, grad_whole)
        grad_hidden = product("rd,fd->rf", grad_whole, weight_down)
        grad_pre = jax.vjp(gelu_exact, pre_act)[1](grad_hidden)[0].astype(jnp.bfloat16)
        grad_up = product("rd,rf->df", whole_in, grad_pre)
        grad_in = collect_grad(product("rf,df->rd", grad_pre, weight_up))
        return (grad_in, grad_up, grad_down)

    def attention_back(
        grad_resid, whole_in, head_rows, att_rows, log_sum, allowed, weight_proj, weight_mix
    ):
        row_count = head_rows.shape[0]
        grad_whole = spread_grad(grad_resid.astype(jnp.bfloat16))
        grad_mix = product("rk,rd->kd", att_rows, grad_whole)
        grad_att = product("rd,kd->rk", grad_whole, weight_mix).astype(jnp.bfloat16)
        grad_att = grad_att.reshape(row_count, local_heads, HD)
        grad_query, grad_key, grad_value = attend_back(
            head_rows[:, :, 0], head_rows[:, :, 1], head_rows[:, :, 2], allowed, log_sum, grad_att
        )
        grad_heads = jnp.stack((grad_query, grad_key, grad_value), axis=2).astype(jnp.bfloat16)
        grad_heads = grad_heads.reshape(row_count, local_heads * 3 * HD)
        grad_proj = product("rd,rk->dk", whole_in, grad_heads)
        grad_in = collect_grad(product("rk,dk->rd", grad_heads, weight_proj))
        return (grad_in, grad_proj, grad_mix)

    resid_zero = patches.astype(jnp.float32)
    normed_one, scaled_one, inv_one = norm_rows(resid_zero, image_norm)
    own_one = normed_one.astype(jnp.bfloat16)
    whole_one = spread(own_one)
    image_heads = product("rd,dk->rk", whole_one, image_proj).astype(jnp.bfloat16)
    image_heads = image_heads.reshape(group_rows, local_heads, 3, HD)
    image_att, image_lse = attend_forward(
        image_heads[:, :, 0], image_heads[:, :, 1], image_heads[:, :, 2], same_image
    )
    image_att = image_att.astype(jnp.bfloat16).reshape(group_rows, local_heads * HD)
    resid_one = resid_zero + collect(product("rk,kd->rd", image_att, image_mix))
    normed_two, scaled_two, inv_two = norm_rows(resid_one, image_ffnorm)
    own_two = normed_two.astype(jnp.bfloat16)
    whole_two = spread(own_two)
    image_pre = product("rd,df->rf", whole_two, image_up)
    image_hidden = gelu_exact(image_pre).astype(jnp.bfloat16)
    resid_two = resid_one + collect(product("rf,fd->rd", image_hidden, image_down))
    embed_own = resid_two.astype(jnp.bfloat16)
    embed_whole = spread(embed_own)
    text_zero = captions.astype(jnp.float32)
    normed_three, scaled_three, inv_three = norm_rows(text_zero, text_norm)
    own_three = normed_three.astype(jnp.bfloat16)
    whole_three = spread(own_three)
    text_heads = product("rd,dk->rk", whole_three, text_proj).astype(jnp.bfloat16)
    text_heads = text_heads.reshape(text_rows, local_heads, 3, HD)
    self_att, self_lse = attend_forward(
        text_heads[:, :, 0], text_heads[:, :, 1], text_heads[:, :, 2], causal
    )
    self_att = self_att.astype(jnp.bfloat16).reshape(text_rows, local_heads * HD)
    text_one = text_zero + collect(product("rk,kd->rd", self_att, text_mix))
    normed_four, scaled_four, inv_four = norm_rows(text_one, cross_norm)
    own_four = normed_four.astype(jnp.bfloat16)
    whole_four = spread(own_four)
    cross_rows = product("rd,dk->rk", whole_four, cross_query).astype(jnp.bfloat16)
    cross_rows = cross_rows.reshape(text_rows, local_heads, HD)
    keyval_rows = product("rd,dk->rk", embed_whole, cross_keyval).astype(jnp.bfloat16)
    keyval_rows = keyval_rows.reshape(group_rows, local_heads, 2, HD)
    cross_att, cross_lse = attend_forward(
        cross_rows, keyval_rows[:, :, 0], keyval_rows[:, :, 1], cross_allowed
    )
    cross_att = cross_att.astype(jnp.bfloat16).reshape(text_rows, local_heads * HD)
    text_two = text_one + collect(product("rk,kd->rd", cross_att, cross_mix))
    normed_five, scaled_five, inv_five = norm_rows(text_two, text_ffnorm)
    own_five = normed_five.astype(jnp.bfloat16)
    whole_five = spread(own_five)
    text_pre = product("rd,df->rf", whole_five, text_up)
    text_hidden = gelu_exact(text_pre).astype(jnp.bfloat16)
    text_three = text_two + collect(product("rf,fd->rd", text_hidden, text_down))
    text_embed = text_three.astype(jnp.bfloat16)
    grad_text = text_cotan.astype(jnp.float32)
    grad_in, grad_text_up, grad_text_down = feed_back(
        grad_text, normed_rows(own_five), text_pre, text_hidden, text_up, text_down
    )
    grad_part, gain_five = norm_back(grad_in, scaled_five, inv_five, text_ffnorm)
    grad_text = grad_text + grad_part
    grad_whole = spread_grad(grad_text.astype(jnp.bfloat16))
    grad_cross_mix = product("rk,rd->kd", cross_att, grad_whole)
    grad_att = product("rd,kd->rk", grad_whole, cross_mix).astype(jnp.bfloat16)
    grad_att = grad_att.reshape(text_rows, local_heads, HD)
    grad_query, grad_key, grad_value = attend_back(
        cross_rows, keyval_rows[:, :, 0], keyval_rows[:, :, 1], cross_allowed, cross_lse, grad_att
    )
    grad_query_rows = grad_query.astype(jnp.bfloat16).reshape(text_rows, local_heads * HD)
    grad_keyval_rows = jnp.stack((grad_key, grad_value), axis=2).astype(jnp.bfloat16)
    grad_keyval_rows = grad_keyval_rows.reshape(group_rows, local_heads * 2 * HD)
    grad_cross_query = product("rd,rk->dk", normed_rows(own_four), grad_query_rows)
    grad_cross_keyval = product("rd,rk->dk", normed_rows(embed_own), grad_keyval_rows)
    grad_in = collect_grad(product("rk,dk->rd", grad_query_rows, cross_query))
    grad_embed = collect_grad(product("rk,dk->rd", grad_keyval_rows, cross_keyval))
    grad_part, gain_four = norm_back(grad_in, scaled_four, inv_four, cross_norm)
    grad_text = grad_text + grad_part
    grad_in, grad_text_proj, grad_text_mix = attention_back(
        grad_text,
        normed_rows(own_three),
        text_heads,
        self_att,
        self_lse,
        causal,
        text_proj,
        text_mix,
    )
    grad_part, gain_three = norm_back(grad_in, scaled_three, inv_three, text_norm)
    grad_text = grad_text + grad_part
    grad_image = image_cotan.astype(jnp.float32) + grad_embed
    grad_in, grad_image_up, grad_image_down = feed_back(
        grad_image, normed_rows(own_two), image_pre, image_hidden, image_up, image_down
    )
    grad_part, gain_two = norm_back(grad_in, scaled_two, inv_two, image_ffnorm)
    grad_image = grad_image + grad_part
    grad_in, grad_image_proj, grad_image_mix = attention_back(
        grad_image,
        normed_rows(own_one),
        image_heads,
        image_att,
        image_lse,
        same_image,
        image_proj,
        image_mix,
    )
    grad_part, gain_one = norm_back(grad_in, scaled_one, inv_one, image_norm)
    grad_image = grad_image + grad_part
    summed = lax.psum(
        (
            grad_image_proj,
            grad_image_mix,
            grad_image_up,
            grad_image_down,
            grad_text_proj,
            grad_text_mix,
            grad_cross_query,
            grad_cross_keyval,
            grad_cross_mix,
            grad_text_up,
            grad_text_down,
            jnp.stack((gain_one, gain_two, gain_three, gain_four, gain_five)),
        ),
        "dp",
    )
    weight_sums = tuple(summed[:11])
    gain_rows = summed[11]
    gain_total = lax.psum(gain_rows, "mp")
    return (
        embed_own,
        text_embed,
        grad_image.astype(jnp.bfloat16),
        grad_text.astype(jnp.bfloat16),
        gain_total[0],
        gain_total[1],
        gain_total[2],
        gain_total[3],
        gain_total[4],
        weight_sums[0],
        weight_sums[1],
        weight_sums[2],
        weight_sums[3],
        weight_sums[4],
        weight_sums[5],
        weight_sums[6],
        weight_sums[7],
        weight_sums[8],
        weight_sums[9],
        weight_sums[10],
    )


def solution(mesh):
    return jax.shard_map(
        local,
        mesh=mesh,
        in_specs=(
            P(("dp", "mp"), None),
            P(("dp", "mp"), None),
            P("dp"),
            P("dp"),
            P(),
            P(),
            P(),
            P(),
            P(),
            P(None, "mp"),
            P("mp", None),
            P(None, "mp"),
            P("mp", None),
            P(None, "mp"),
            P("mp", None),
            P(None, "mp"),
            P(None, "mp"),
            P("mp", None),
            P(None, "mp"),
            P("mp", None),
            P(("dp", "mp"), None),
            P(("dp", "mp"), None),
        ),
        out_specs=(
            P(("dp", "mp"), None),
            P(("dp", "mp"), None),
            P(("dp", "mp"), None),
            P(("dp", "mp"), None),
            P(),
            P(),
            P(),
            P(),
            P(),
            P(None, "mp"),
            P("mp", None),
            P(None, "mp"),
            P("mp", None),
            P(None, "mp"),
            P("mp", None),
            P(None, "mp"),
            P(None, "mp"),
            P("mp", None),
            P(None, "mp"),
            P("mp", None),
        ),
        check_vma=False,
    )
```

profile of v0, /device:TPU:0, one launch (start us, length us, event | category | flops | bytes accessed | tf_op | source)
XLA Modules:
  0.0 1313.9 jit_solution(9574013306389608256)
XLA Ops:
  12.0 25.9 %all-gather.6.cloned.1.call-done = bf16[784,768]{1,0:T(8,128)(2,1)} async-done(((bf16[392,768]{1,0:T(8,128)(2,1)}), bf16[784,768]{1,0:T(8,128)(2,1)}) %all-gather.6.cloned.1.call-update) | async-done | bytes 1204240 | tf_op jit(solution)/shard_map/all_gather | solution.py:118
  57.3 38.1 %while.84 = (s32[]{:T(128)}, bf16[6,784,64]{1,2,0:T(8,128)(2,1)}, f32[6,784]{1,0:T(8,128)}, bf16[6,784,64]{2,1,0:T(8,128)(2,1)}, bf16[6,784,64]{2,1,0:T(8,128)(2...) while((s32[]{:T(128)}, bf16[6,784,64]{1,2,0:T(8,128)(2,1)}, ...), condition=%wide.region_5.6_spmd.clone, body=%wide.region_2.5_spmd.clone.sunk | while | flops 166570992 | bytes 8619817 | solution.py:57
  100.2 34.2 %reduce-scatter.12.cloned.1.call-done = f32[392,768]{1,0:T(8,128)} async-done(((f32[784,768]{1,0:T(8,128)}), f32[392,768]{1,0:T(8,128)}) %reduce-scatter.12.cloned.1.call-update) | async-done | bytes 1204240 | tf_op jit(solution)/shard_map/reduce_scatter | solution.py:121
  138.3 7.6 all_gather.41
  161.2 14.8 %multiply_convert_fusion.3 = (bf16[784,1536]{1,0:T(8,128)(2,1)S(1)}, f32[784,1536]{1,0:T(8,128)}, f32[784,1536]{1,0:T(8,128)}) fusion(bf16[784,768]{1,0:T(8,128)(2,1)} %all-gather.8.cloned.1.call-done, bf16[768,1536]{1,0:T(8,128)(2,1)S(1)} %copy-done), kind=kOutput, calls=%fused_computation.173 | convolution fusion | flops 1927962624 | bytes 15605760 | tf_op jit(solution)/shard_map/rd,df->rf/dot_general | solution.py:36
  181.0 13.9 %while.85 = (s32[]{:T(128)}, bf16[6,256,64]{1,2,0:T(8,128)(2,1)S(1)}, f32[6,256]{1,0:T(8,128)S(1)}, bf16[6,256,64]{2,1,0:T(8,128)(2,1)}, bf16[6,256,64]{2,1,0:T(...) while((s32[]{:T(128)}, ...), condition=%wide.region_15.16_spmd.clone, body=%wide.region_12.15_spmd.clone.sunk | while | flops 17497856 | bytes 1063017 | solution.py:57
  196.9 19.5 %reduce-scatter.14.cloned.1.call-done = f32[392,768]{1,0:T(8,128)} async-done(((f32[784,768]{1,0:T(8,128)}), f32[392,768]{1,0:T(8,128)}) %reduce-scatter.14.cloned.1.call-update) | async-done | bytes 1204240 | tf_op jit(solution)/shard_map/reduce_scatter | solution.py:121
  219.1 17.5 %reduce-scatter.16.cloned.1.call-done = f32[128,768]{1,0:T(8,128)} async-done(((f32[256,768]{1,0:T(8,128)}), f32[128,768]{1,0:T(8,128)}) %reduce-scatter.16.cloned.1.call-update) | async-done | bytes 393232 | tf_op jit(solution)/shard_map/reduce_scatter | solution.py:121
  248.9 12.8 all-gather.10.cloned.1.call-done
  275.6 23.9 %while.86 = (s32[]{:T(128)}, bf16[6,256,64]{1,2,0:T(8,128)(2,1)S(1)}, f32[6,256]{1,0:T(8,128)}, bf16[6,256,64]{2,1,0:T(8,128)(2,1)S(1)}, bf16[6,784,64]{2,1,0:T(...) while((s32[]{:T(128)}, ...), condition=%wide.region_22.23_spmd.clone, body=%wide.region_19.22_spmd.clone.sunk | while | flops 53186304 | bytes 2958449 | solution.py:57
  302.2 8.4 all_gather.45
  310.6 9.2 reduce-scatter.18.cloned.1.call-done
  344.4 13.6 %reduce-scatter.22.cloned.1.call-done = f32[128,768]{1,0:T(8,128)} async-done(((f32[256,768]{1,0:T(8,128)}), f32[128,768]{1,0:T(8,128)}) %reduce-scatter.22.cloned.1.call-update) | async-done | bytes 393232 | tf_op jit(solution)/shard_map/reduce_scatter | solution.py:127
  360.4 18.0 %reduce-scatter.20.cloned.1.call-done = f32[128,768]{1,0:T(8,128)} async-done(((f32[256,768]{1,0:T(8,128)}), f32[128,768]{1,0:T(8,128)}) %reduce-scatter.20.cloned.1.call-update) | async-done | bytes 393232 | tf_op jit(solution)/shard_map/reduce_scatter | solution.py:121
  390.8 47.8 %while.87 = (s32[]{:T(128)}, bf16[6,256,64]{1,2,0:T(8,128)(2,1)S(1)}, bf16[6,784,64]{1,2,0:T(8,128)(2,1)}, bf16[6,784,64]{1,2,0:T(8,128)(2,1)}, bf16[6,256,64]{2...) while((s32[]{:T(128)}, ...), condition=%wide.region_32.33_spmd.clone, body=%wide.region_30.32_spmd.clone.sunk | while | flops 130523904 | bytes 7358657 | solution.py:79
  444.7 35.4 %reduce-scatter.24.cloned.1.call-done = f32[392,768]{1,0:T(8,128)} async-done(((f32[784,768]{1,0:T(8,128)}), f32[392,768]{1,0:T(8,128)}) %reduce-scatter.24.cloned.1.call-update) | async-done | bytes 1204240 | tf_op jit(solution)/shard_map/reduce_scatter | solution.py:127
  485.0 20.7 %all-gather.12.cloned.1.call-done = bf16[784,768]{1,0:T(8,128)(2,1)} async-done(((bf16[392,768]{1,0:T(8,128)(2,1)}), bf16[784,768]{1,0:T(8,128)(2,1)}) %all-gather.12.cloned.1.call-update) | async-done | bytes 1204240 | tf_op jit(solution)/shard_map/all_gather | solution.py:124
  505.7 8.0 add_convert_fusion
  529.8 8.1 all_gather.49
  538.5 26.1 %reduce-scatter.26.cloned.1.call-done = f32[392,768]{1,0:T(8,128)} async-done(((f32[784,768]{1,0:T(8,128)}), f32[392,768]{1,0:T(8,128)}) %reduce-scatter.26.cloned.1.call-update) | async-done | bytes 1204240 | tf_op jit(solution)/shard_map/reduce_scatter | solution.py:127
  569.7 31.1 %while.89 = (s32[]{:T(128)}, bf16[6,256,64]{1,2,0:T(8,128)(2,1)S(1)}, bf16[6,256,64]{1,2,0:T(8,128)(2,1)S(1)}, bf16[6,256,64]{1,2,0:T(8,128)(2,1)S(1)}, bf16[6,2...) while((s32[]{:T(128)}, ...), condition=%wide.region_48.49_spmd.clone, body=%wide.region_46.48_spmd.clone.sunk | while | flops 42761984 | bytes 2568313 | solution.py:79
  609.4 60.7 %while.88 = (s32[]{:T(128)}, bf16[6,784,64]{1,2,0:T(8,128)(2,1)}, bf16[6,784,64]{1,2,0:T(8,128)(2,1)}, bf16[6,784,64]{1,2,0:T(8,128)(2,1)}, bf16[6,784,64]{2,1,0...) while((s32[]{:T(128)}, bf16[6,784,64]{1,2,0:T(8,128)(2,1)}, ...), condition=%wide.region_39.40_spmd.clone, body=%wide.region_37.39_spmd.clone.sunk | while | flops 399625984 | bytes 21093240 | solution.py:79
  716.0 64.3 %psum.91 = f32[5,768]{1,0:T(8,128)S(1)} all-reduce(f32[5,768]{1,0:T(8,128)S(1)} %stack.78), channel_id=1, replica_groups=mesh['dp'=16,'mp'=2] {'dp'}, use_global_device_ids=true, to_apply=%region_57.58 | all-reduce | flops 3840 | bytes 30720 | tf_op jit(solution)/shard_map/psum | solution.py:272
  790.5 488.7 %all-reduce.3.cloned.1.call-done = (f32[768,1152]{1,0:T(8,128)}, f32[384,768]{1,0:T(8,128)}, f32[768,1536]{1,0:T(8,128)}, f32[1536,768]{1,0:T(8,128)}, f32[768,1...) async-done(((f32[768,1152]{1,0:T(8,128)}, ...) | async-done | bytes 33030160 | tf_op jit(solution)/shard_map/psum | solution.py:272
  (607 shorter events, 464.7 us)
Async XLA Ops:
  7.2 154.0 %copy-start = (bf16[768,1536]{1,0:T(8,128)(2,1)S(1)}, bf16[768,1536]{1,0:T(8,128)(2,1)}, u32[]{:S(2)}) copy-start(bf16[768,1536]{1,0:T(8,128)(2,1)} %param.45) | copy-start | bytes 7077892
  7.2 30.6 %all-gather.6.cloned.1.call-start = ((), (), s32[]{:S(2)}) async-start(), calls=%async_computation.11 | async-start | bytes 1806336 | tf_op jit(solution)/shard_map/all_gather | solution.py:118
  11.9 122.6 %reduce-scatter.12.cloned.1.call-start = ((), (), s32[]{:S(2)}) async-start(), calls=%async_computation.12 | async-start | bytes 3612672 | tf_op jit(solution)/shard_map/reduce_scatter | solution.py:121
  99.0 62.2 %all-gather.8.cloned.1.call-start = ((), (), s32[]{:S(2)}) async-start(), calls=%async_computation.13 | async-start | bytes 1806336 | tf_op jit(solution)/shard_map/all_gather | solution.py:118
  100.0 38.1 %copy-start.73 = (f32[128]{0:T(128)}, f32[128]{0:T(128)S(1)}, u32[]{:S(2)}) copy-start(f32[128]{0:T(128)S(1)} %broadcast_multiply_fusion.14) | copy-start | bytes 1540
  138.0 78.4 %reduce-scatter.14.cloned.1.call-start = ((), (), s32[]{:S(2)}) async-start(), calls=%async_computation.14 | async-start | bytes 3612672 | tf_op jit(solution)/shard_map/reduce_scatter | solution.py:121
  180.9 55.7 %reduce-scatter.16.cloned.1.call-start = ((), (), s32[]{:S(2)}) async-start(), calls=%async_computation.15 | async-start | bytes 1179648 | tf_op jit(solution)/shard_map/reduce_scatter | solution.py:121
  196.2 65.4 %all-gather.10.cloned.1.call-start = ((), (), s32[]{:S(2)}) async-start(), calls=%async_computation.16 | async-start | bytes 1806336 | tf_op jit(solution)/shard_map/all_gather | solution.py:118
  219.0 100.7 %reduce-scatter.18.cloned.1.call-start = ((), (), s32[]{:S(2)}) async-start(), calls=%async_computation.17 | async-start | bytes 1179648 | tf_op jit(solution)/shard_map/reduce_scatter | solution.py:121
  302.1 55.9 %reduce-scatter.22.cloned.1.call-start = ((), (), s32[]{:S(2)}) async-start(), calls=%async_computation.19 | async-start | bytes 1179648 | tf_op jit(solution)/shard_map/reduce_scatter | solution.py:127
  339.5 38.9 %reduce-scatter.20.cloned.1.call-start = ((), (), s32[]{:S(2)}) async-start(), calls=%async_computation.18 | async-start | bytes 1179648 | tf_op jit(solution)/shard_map/reduce_scatter | solution.py:121
  344.4 135.8 %reduce-scatter.24.cloned.1.call-start = ((), (), s32[]{:S(2)}) async-start(), calls=%async_computation.20 | async-start | bytes 3612672 | tf_op jit(solution)/shard_map/reduce_scatter | solution.py:127
  438.6 44.0 %copy-start.34 = (bf16[6,256,64]{1,2,0:T(8,128)(2,1)}, bf16[6,256,64]{1,2,0:T(8,128)(2,1)S(1)}, u32[]{:S(2)}) copy-start(bf16[6,256,64]{1,2,0:T(8,128)(2,1)S(1)} %get-tuple-element.306) | copy-start | bytes 589828
  444.7 61.1 %all-gather.12.cloned.1.call-start = ((), (), s32[]{:S(2)}) async-start(), calls=%async_computation.21 | async-start | bytes 1806336 | tf_op jit(solution)/shard_map/all_gather | solution.py:124
  482.5 43.4 %reduce-scatter.30.cloned.1.call-start = ((), (), s32[]{:S(2)}) async-start(), calls=%async_computation.25 | async-start | bytes 1179648 | tf_op jit(solution)/shard_map/reduce_scatter | solution.py:127
  485.0 79.6 %reduce-scatter.26.cloned.1.call-start = ((), (), s32[]{:S(2)}) async-start(), calls=%async_computation.22 | async-start | bytes 3612672 | tf_op jit(solution)/shard_map/reduce_scatter | solution.py:127
  518.7 85.5 %all-gather.14.cloned.1.call-start = ((), (), s32[]{:S(2)}) async-start(), calls=%async_computation.23 | async-start | bytes 1806336 | tf_op jit(solution)/shard_map/all_gather | solution.py:124
  527.8 36.8 %copy-start.3 = (f32[392,768]{1,0:T(8,128)S(1)}, f32[392,768]{1,0:T(8,128)}, u32[]{:S(2)}) copy-start(f32[392,768]{1,0:T(8,128)} %copy-done.2) | copy-start | bytes 3612676
  527.8 36.8 %copy-start.62 = (f32[768]{0:T(1024)S(1)}, f32[768]{0:T(1024)}, u32[]{:S(2)}) copy-start(f32[768]{0:T(1024)} %param.39) | copy-start | bytes 9220
  527.8 36.8 %copy-start.67 = (f32[392]{0:T(512)S(1)}, f32[392]{0:T(512)}, u32[]{:S(2)}) copy-start(f32[392]{0:T(512)} %copy-done.66) | copy-start | bytes 4708
  569.6 141.1 %reduce-scatter.32.cloned.1.call-start = ((), (), s32[]{:S(2)}) async-start(), calls=%async_computation.26 | async-start | bytes 1179648 | tf_op jit(solution)/shard_map/reduce_scatter | solution.py:127
  604.1 109.9 %reduce-scatter.28.cloned.1.call-start = ((), (), s32[]{:S(2)}) async-start(), calls=%async_computation.24 | async-start | bytes 3612672 | tf_op jit(solution)/shard_map/reduce_scatter | solution.py:127
  677.6 601.6 %all-reduce.3.cloned.1.call-start = ((), (), s32[]{:S(2)}) async-start(), calls=%async_computation.27 | async-start | bytes 66060288 | tf_op jit(solution)/shard_map/psum | solution.py:272
  712.0 75.9 %copy-start.11 = (f32[392,768]{1,0:T(8,128)S(1)}, f32[392,768]{1,0:T(8,128)}, u32[]{:S(2)}) copy-start(f32[392,768]{1,0:T(8,128)} %get-tuple-element.630) | copy-start | bytes 3612676
  (94 other events, 641.7 us)
Sparse Core Ops, SparseCore 0:
  12.0 25.7 all-gather.5
  99.1 35.2 reduce-scatter.11
  138.2 23.0 all-gather.7
  181.1 35.3 reduce-scatter.13
  219.1 17.4 reduce-scatter.15
  238.6 23.0 all-gather.9
  302.2 17.4 reduce-scatter.17
  339.6 18.3 reduce-scatter.21
  360.8 17.5 reduce-scatter.19
  444.8 35.3 reduce-scatter.23
  482.7 23.0 all-gather.11
  508.4 17.4 reduce-scatter.29
  528.8 35.7 reduce-scatter.25
  569.7 23.0 all-gather.13
  604.3 17.5 reduce-scatter.31
  677.7 35.3 reduce-scatter.27
  720.5 558.5 all-reduce.2
where the time goes:
time: 1330 us; the launch traced here: 1310 us
  waiting for transfers between devices  734 us (55%)
  matrix products  279 us (21%)
  blocking collectives  117 us (9%)
  local copies, waits for them, and re-layouts  113 us (8%)
  other arithmetic  52.9 us (4%)
  between operations  15.4 us (1%)
    psum x1, waiting for transfers between devices, local(): lax.psum((grad_image_proj, grad_image_mix, grad_image_up, grad_image_down...  489 us
    dot_general x123, matrix products, product(): return jnp.einsum(form, left, right, preferred_element_type=jnp.float32)  224 us
    reduce_scatter x5, waiting for transfers between devices, collect(): return lax.psum_scatter(partial_rows, 'mp', scatter_dimension=0, tiled=True)  98.5 us
    reduce_scatter x6, waiting for transfers between devices, collect_grad(): return lax.psum_scatter(partial_rows, 'mp', scatter_dimension=0, tiled=True)  82.3 us
    psum x1, blocking collectives, local(): lax.psum((grad_image_proj, grad_image_mix, grad_image_up, grad_image_down...  64.3 us
    unnamed x222, local copies, waits for them, and re-layouts  59.9 us
    all_gather x3, waiting for transfers between devices, spread(): return lax.all_gather(own_rows, 'mp', axis=0, tiled=True)  43.9 us
    dot_general x18, matrix products, per_head(): jnp.dot(probability, value_head, preferred_element_type=jnp.float32)  29.3 us
  transfers between devices with their start and end apart: 17, of which 14 were waited for; matrix products, arithmetic and copies ran while one was open for 15% of the time, Pallas kernels for 0%

commit v1 on v0

v1 whole, which is shorter than its diff:
```python
import functools

import jax
import jax.numpy as jnp
from jax import lax
from jax.experimental import pallas as pl
from jax.experimental.pallas import tpu as pltpu
from jax.sharding import PartitionSpec as P

HD = 64
LT = 128
NEG_FILL = -1000000000.0
EPS = 1e-06
F32 = jnp.float32
BF16 = jnp.bfloat16
SCALE = HD**-0.5
VMEM_LIMIT = 56 * 2**20


def mm(left, right, left_dim, right_dim, **options):
    return lax.dot_general(
        left,
        right,
        (((left_dim,), (right_dim,)), ((), ())),
        preferred_element_type=F32,
        **options,
    )


def row_step(rows):
    return 112 if rows % 112 == 0 else 128


def over_rows(rows, body):
    step = row_step(rows)

    @pl.loop(0, rows // step)
    def _(i):
        body(pl.ds(pl.multiple_of(i * step, 16), step))


def norm_parts(values):
    centred = values - jnp.mean(values, axis=-1, keepdims=True)
    inv_std = lax.rsqrt(jnp.mean(centred * centred, axis=-1, keepdims=True) + EPS)
    return centred * inv_std, inv_std


def norm_back(grad_out, scaled, inv_std, gain):
    grad_scaled = grad_out * gain
    mean_grad = jnp.mean(grad_scaled, axis=-1, keepdims=True)
    mean_cross = jnp.mean(grad_scaled * scaled, axis=-1, keepdims=True)
    return inv_std * (grad_scaled - mean_grad - scaled * mean_cross)


def total(refs, rows):
    value = refs[0][rows].astype(F32)
    for ref in refs[1:]:
        value = value + ref[rows].astype(F32)
    return value


def gelu_both(values):
    half = 0.5 * (1.0 + lax.erf(values * (0.5**0.5)))
    density = jnp.exp(-0.5 * values * values) * ((0.5 / jnp.pi) ** 0.5)
    return values * half, half + values * density


def allowed_of(key_ref, query_ref, causal):
    allowed = key_ref[...] == query_ref[...]
    if causal:
        key_row = lax.broadcasted_iota(jnp.int32, allowed.shape, 0)
        query_row = lax.broadcasted_iota(jnp.int32, allowed.shape, 1)
        allowed = allowed & (key_row <= query_row)
    return allowed


def attend_pair(heads, allowed, lse_ref):
    outs = []
    for h, (query, key, value) in enumerate(heads):
        scores = jnp.where(allowed, mm(key, query, 1, 1), NEG_FILL)
        top = jnp.max(scores, axis=0, keepdims=True)
        weight = jnp.exp(scores - top).astype(BF16)
        with_ones = jnp.concatenate((value, jnp.ones(value.shape, BF16)), axis=1)
        result = mm(with_ones, weight, 0, 0)
        sums = result[HD : HD + 1]
        outs.append(result[:HD] / sums)
        lse_ref[0, h : h + 1] = top + jnp.log(sums)
    return jnp.concatenate(outs, axis=0).T.astype(BF16)


def attend_pair_back(heads, allowed, lse_ref, att, grad_att):
    product = grad_att.astype(F32) * att.astype(F32)
    lane = lax.broadcasted_iota(jnp.int32, (8, 2 * HD), 1)
    line = lax.broadcasted_iota(jnp.int32, (8, 2 * HD), 0)
    pick = jnp.where(lane // HD == line, 1.0, 0.0).astype(F32)
    row_dots = mm(pick, product, 1, 1, precision=lax.Precision.HIGHEST)
    grad_queries, rest = [], []
    for h, (query, key, value) in enumerate(heads):
        grad_head = grad_att[:, h * HD : (h + 1) * HD]
        scores = jnp.where(allowed, mm(key, query, 1, 1), NEG_FILL)
        prob = jnp.exp(scores - lse_ref[0, h : h + 1])
        grad_value = mm(prob.astype(BF16), grad_head, 1, 0)
        grad_prob = mm(value, grad_head, 1, 1)
        grad_scores = (prob * (grad_prob - row_dots[h : h + 1])).astype(BF16)
        rest.append((mm(grad_scores, query, 1, 0), grad_value))
        grad_queries.append(mm(key, grad_scores, 0, 0))
    return jnp.concatenate(grad_queries, axis=0).T * SCALE, rest


def split_heads(block):
    factor = jnp.asarray(SCALE, BF16)
    heads = []
    for h in range(2):
        query, key, value = (
            block[:, (3 * h + j) * HD : (3 * h + j + 1) * HD] for j in range(3)
        )
        heads.append((query * factor, key, value))
    return heads


def split_cross(query_block, keyval_block):
    factor = jnp.asarray(SCALE, BF16)
    return [
        (
            query_block[:, h * HD : (h + 1) * HD] * factor,
            keyval_block[:, 2 * h * HD : (2 * h + 1) * HD],
            keyval_block[:, (2 * h + 1) * HD : (2 * h + 2) * HD],
        )
        for h in range(2)
    ]


def whole(shape):
    return pl.BlockSpec(shape, lambda i: (0,) * len(shape), pipeline_mode=pl.Buffered(1))


def columns(rows, width):
    return pl.BlockSpec((rows, width), lambda i: (0, i))


def lines(height, width):
    return pl.BlockSpec((height, width), lambda i: (i, 0))


def per_pair(rows):
    return pl.BlockSpec((1, 2, rows), lambda i: (i, 0, 0))


def out(shape, dtype):
    return jax.ShapeDtypeStruct(shape, dtype)


def call(kernel, name, steps, ins, outs, scratch, args, flops):
    size = sum(a.size * a.dtype.itemsize for a in args)
    size += sum(o.size * o.dtype.itemsize for o, _ in outs)
    return pl.pallas_call(
        kernel,
        name=name,
        grid=(steps,),
        in_specs=ins,
        out_specs=[spec for _, spec in outs],
        out_shape=[shape for shape, _ in outs],
        scratch_shapes=scratch,
        compiler_params=pltpu.CompilerParams(vmem_limit_bytes=VMEM_LIMIT),
        cost_estimate=pl.CostEstimate(flops=flops, bytes_accessed=size, transcendentals=0),
    )(*args)


def self_forward(rows_in, gain, proj, mix, ids, causal, name):
    rows, width = rows_in.shape
    pairs = mix.shape[0] // (2 * HD)

    def kernel(x, g, w, m, kid, qid, normed, qkv, att, lse, part, acc):
        step = pl.program_id(0)

        @pl.when(step == 0)
        def _():
            def body(at):
                scaled, _ = norm_parts(x[at].astype(F32))
                normed[at] = (scaled * g[...]).astype(BF16)

            over_rows(rows, body)

        block = mm(normed[...], w[...], 1, 0).astype(BF16)
        qkv[...] = block
        result = attend_pair(split_heads(block), allowed_of(kid, qid, causal), lse)
        att[...] = result
        share = mm(result, m[...], 1, 0)

        @pl.when(step == 0)
        def _():
            acc[...] = share

        @pl.when((step > 0) & (step < pairs - 1))
        def _():
            acc[...] += share

        @pl.when(step == pairs - 1)
        def _():
            part[...] = (acc[...] + share).astype(BF16)

    flops = 2 * rows * (width * (4 * pairs * 2 * HD) + rows * pairs * 4 * HD)
    return call(
        kernel,
        name,
        pairs,
        [
            whole((rows, width)),
            whole((1, width)),
            columns(width, 6 * HD),
            lines(2 * HD, width),
            whole((rows, 1)),
            whole((1, rows)),
        ],
        [
            (out((rows, width), BF16), whole((rows, width))),
            (out((rows, pairs * 6 * HD), BF16), columns(rows, 6 * HD)),
            (out((rows, pairs * 2 * HD), BF16), columns(rows, 2 * HD)),
            (out((pairs, 2, rows), F32), per_pair(rows)),
            (out((rows, width), BF16), whole((rows, width))),
        ],
        [pltpu.VMEM((rows, width), F32)],
        (rows_in, gain.reshape(1, width), proj, mix, ids.reshape(rows, 1), ids.reshape(1, rows)),
        flops,
    )


def feed_forward(pieces, gain, up, down, name):
    rows, width = pieces[0].shape
    hidden = up.shape[1]
    block = 256
    steps = hidden // block
    count = len(pieces)

    def kernel(*refs):
        parts = refs[:count]
        g, u, d, mid, normed, hid, slope, part, acc = refs[count:]
        step = pl.program_id(0)

        @pl.when(step == 0)
        def _():
            def body(at):
                value = total(parts, at)
                mid[at] = value
                scaled, _ = norm_parts(value)
                normed[at] = (scaled * g[...]).astype(BF16)

            over_rows(rows, body)

        value, derivative = gelu_both(mm(normed[...], u[...], 1, 0))
        value = value.astype(BF16)
        hid[...] = value
        slope[...] = derivative.astype(BF16)
        share = mm(value, d[...], 1, 0)

        @pl.when(step == 0)
        def _():
            acc[...] = share

        @pl.when((step > 0) & (step < steps - 1))
        def _():
            acc[...] += share

        @pl.when(step == steps - 1)
        def _():
            part[...] = (acc[...] + share).astype(BF16)

    return call(
        kernel,
        name,
        steps,
        [whole((rows, width))] * count
        + [whole((1, width)), columns(width, block), lines(block, width)],
        [
            (out((rows, width), F32), whole((rows, width))),
            (out((rows, width), BF16), whole((rows, width))),
            (out((rows, hidden), BF16), columns(rows, block)),
            (out((rows, hidden), BF16), columns(rows, block)),
            (out((rows, width), BF16), whole((rows, width))),
        ],
        [pltpu.VMEM((rows, width), F32)],
        (*pieces, gain.reshape(1, width), up, down),
        4 * rows * width * hidden,
    )


def cross_forward(image_pieces, text_pieces, gain, query_w, keyval_w, mix, key_id, query_id):
    keys, width = image_pieces[0].shape
    rows = text_pieces[0].shape[0]
    pairs = mix.shape[0] // (2 * HD)
    n_image, n_text = len(image_pieces), len(text_pieces)

    def kernel(*refs):
        image = refs[:n_image]
        text = refs[n_image : n_image + n_text]
        g, wq, wkv, m, kid, qid = refs[n_image + n_text : n_image + n_text + 6]
        embed, mid, normed, q, kv, att, lse, part, acc = refs[n_image + n_text + 6 :]
        step = pl.program_id(0)

        @pl.when(step == 0)
        def _():
            def image_body(at):
                embed[at] = total(image, at).astype(BF16)

            over_rows(keys, image_body)

            def text_body(at):
                value = total(text, at)
                mid[at] = value
                scaled, _ = norm_parts(value)
                normed[at] = (scaled * g[...]).astype(BF16)

            over_rows(rows, text_body)

        query_block = mm(normed[...], wq[...], 1, 0).astype(BF16)
        keyval_block = mm(embed[...], wkv[...], 1, 0).astype(BF16)
        q[...] = query_block
        kv[...] = keyval_block
        result = attend_pair(
            split_cross(query_block, keyval_block), allowed_of(kid, qid, False), lse
        )
        att[...] = result
        share = mm(result, m[...], 1, 0)

        @pl.when(step == 0)
        def _():
            acc[...] = share

        @pl.when((step > 0) & (step < pairs - 1))
        def _():
            acc[...] += share

        @pl.when(step == pairs - 1)
        def _():
            part[...] = (acc[...] + share).astype(BF16)

    flops = 2 * pairs * 2 * HD * (width * (2 * rows + 2 * keys) + 2 * rows * keys)
    return call(
        kernel,
        "cross_forward",
        pairs,
        [whole((keys, width))] * n_image
        + [whole((rows, width))] * n_text
        + [
            whole((1, width)),
            columns(width, 2 * HD),
            columns(width, 4 * HD),
            lines(2 * HD, width),
            whole((keys, 1)),
            whole((1, rows)),
        ],
        [
            (out((keys, width), BF16), whole((keys, width))),
            (out((rows, width), F32), whole((rows, width))),
            (out((rows, width), BF16), whole((rows, width))),
            (out((rows, pairs * 2 * HD), BF16), columns(rows, 2 * HD)),
            (out((keys, pairs * 4 * HD), BF16), columns(keys, 4 * HD)),
            (out((rows, pairs * 2 * HD), BF16), columns(rows, 2 * HD)),
            (out((pairs, 2, rows), F32), per_pair(rows)),
            (out((rows, width), BF16), whole((rows, width))),
        ],
        [pltpu.VMEM((rows, width), F32)],
        (
            *image_pieces,
            *text_pieces,
            gain.reshape(1, width),
            query_w,
            keyval_w,
            mix,
            key_id.reshape(keys, 1),
            query_id.reshape(1, rows),
        ),
        flops,
    )


def feed_both(pieces, cotan, gain, up, down):
    rows, width = pieces[0].shape
    hidden = up.shape[1]
    block = 256
    steps = hidden // block
    count = len(pieces)

    def kernel(*refs):
        parts = refs[:count]
        gy, g, u, d, mid, normed, hid, dpre, part, dpart, acc, dacc = refs[count:]
        step = pl.program_id(0)

        @pl.when(step == 0)
        def _():
            def body(at):
                value = total(parts, at)
                mid[at] = value
                scaled, _ = norm_parts(value)
                normed[at] = (scaled * g[...]).astype(BF16)

            over_rows(rows, body)
            acc[...] = jnp.zeros_like(acc)
            dacc[...] = jnp.zeros_like(dacc)

        value, derivative = gelu_both(mm(normed[...], u[...], 1, 0))
        value = value.astype(BF16)
        hid[...] = value
        acc[...] += mm(value, d[...], 1, 0)
        grad_pre = (mm(gy[...], d[...], 1, 1) * derivative).astype(BF16)
        dpre[...] = grad_pre
        dacc[...] += mm(grad_pre, u[...], 1, 1)

        @pl.when(step == steps - 1)
        def _():
            part[...] = acc[...].astype(BF16)
            dpart[...] = dacc[...].astype(BF16)

    return call(
        kernel,
        "text_feed",
        steps,
        [whole((rows, width))] * (count + 1)
        + [whole((1, width)), columns(width, block), lines(block, width)],
        [
            (out((rows, width), F32), whole((rows, width))),
            (out((rows, width), BF16), whole((rows, width))),
            (out((rows, hidden), BF16), columns(rows, block)),
            (out((rows, hidden), BF16), columns(rows, block)),
            (out((rows, width), BF16), whole((rows, width))),
            (out((rows, width), BF16), whole((rows, width))),
        ],
        [pltpu.VMEM((rows, width), F32)] * 2,
        (*pieces, cotan, gain.reshape(1, width), up, down),
        8 * rows * width * hidden,
    )


def norm_back_rows(rows, grads, mid, gain, upper, grad_sum, grad_low, gain_grad):
    gain_grad[...] = jnp.zeros_like(gain_grad)

    def body(at):
        grad = total(grads, at)
        scaled, inv_std = norm_parts(mid[at])
        gain_grad[...] += jnp.sum(grad * scaled, axis=0, keepdims=True)
        value = total(upper, at) + norm_back(grad, scaled, inv_std, gain[...])
        grad_sum[at] = value
        grad_low[at] = value.astype(BF16)

    over_rows(rows, body)


def cross_back(upper, grads, mid, gain, q, kv, att, lse, query_w, keyval_w, mix, key_id, query_id):
    rows, width = mid.shape
    keys = kv.shape[0]
    pairs = mix.shape[0] // (2 * HD)

    def kernel(up0, g0, g1, md, g, qr, kvr, ar, lr, wq, wkv, m, kid, qid, *rest):
        gsum, glow, ggain, dq, dkv, dpart, epart, dacc, eacc = rest
        step = pl.program_id(0)

        @pl.when(step == 0)
        def _():
            norm_back_rows(rows, (g0, g1), md, g, (up0,), gsum, glow, ggain)
            dacc[...] = jnp.zeros_like(dacc)
            eacc[...] = jnp.zeros_like(eacc)

        grad_att = mm(glow[...], m[...], 1, 1).astype(BF16)
        grad_query, rest_pair = attend_pair_back(
            split_cross(qr[...], kvr[...]), allowed_of(kid, qid, False), lr, ar[...], grad_att
        )
        grad_query = grad_query.astype(BF16)
        dq[...] = grad_query
        grad_keyval = jnp.concatenate([piece for pair in rest_pair for piece in pair], axis=1)
        grad_keyval = grad_keyval.astype(BF16)
        dkv[...] = grad_keyval
        dacc[...] += mm(grad_query, wq[...], 1, 1)
        eacc[...] += mm(grad_keyval, wkv[...], 1, 1)

        @pl.when(step == pairs - 1)
        def _():
            dpart[...] = dacc[...].astype(BF16)
            epart[...] = eacc[...].astype(BF16)

    flops = 2 * pairs * 2 * HD * (width * (2 * rows + 2 * keys) + 5 * rows * keys)
    return call(
        kernel,
        "cross_back",
        pairs,
        [whole((rows, width))] * 4
        + [
            whole((1, width)),
            columns(rows, 2 * HD),
            columns(keys, 4 * HD),
            columns(rows, 2 * HD),
            per_pair(rows),
            columns(width, 2 * HD),
            columns(width, 4 * HD),
            lines(2 * HD, width),
            whole((keys, 1)),
            whole((1, rows)),
        ],
        [
            (out((rows, width), F32), whole((rows, width))),
            (out((rows, width), BF16), whole((rows, width))),
            (out((1, width), F32), whole((1, width))),
            (out(q.shape, BF16), columns(rows, 2 * HD)),
            (out(kv.shape, BF16), columns(keys, 4 * HD)),
            (out((rows, width), BF16), whole((rows, width))),
            (out((keys, width), BF16), whole((keys, width))),
        ],
        [pltpu.VMEM((rows, width), F32), pltpu.VMEM((keys, width), F32)],
        (
            upper,
            *grads,
            mid,
            gain.reshape(1, width),
            q,
            kv,
            att,
            lse,
            query_w,
            keyval_w,
            mix,
            key_id.reshape(keys, 1),
            query_id.reshape(1, rows),
        ),
        flops,
    )


def self_back(upper, grads, mid, gain, qkv, att, lse, proj, mix, ids, causal, rows_in, name):
    rows, width = mid.shape
    pairs = mix.shape[0] // (2 * HD)

    def kernel(up0, g0, g1, md, g, qr, ar, lr, w, m, kid, qid, x, *rest):
        gsum, glow, ggain, dqkv, dpart, igain, dacc = rest
        step = pl.program_id(0)

        @pl.when(step == 0)
        def _():
            norm_back_rows(rows, (g0, g1), md, g, (up0,), gsum, glow, ggain)
            dacc[...] = jnp.zeros_like(dacc)

        grad_att = mm(glow[...], m[...], 1, 1).astype(BF16)
        grad_query, pair = attend_pair_back(
            split_heads(qr[...]), allowed_of(kid, qid, causal), lr, ar[...], grad_att
        )
        grad_block = jnp.concatenate(
            [grad_query[:, :HD], *pair[0], grad_query[:, HD:], *pair[1]], axis=1
        ).astype(BF16)
        dqkv[...] = grad_block
        dacc[...] += mm(grad_block, w[...], 1, 1)

        @pl.when(step == pairs - 1)
        def _():
            igain[...] = jnp.zeros_like(igain)

            def body(at):
                grad = dacc[at]
                scaled, _ = norm_parts(x[at].astype(F32))
                igain[...] += jnp.sum(grad * scaled, axis=0, keepdims=True)
                dpart[at] = grad.astype(BF16)

            over_rows(rows, body)

    flops = 2 * rows * pairs * 2 * HD * (width * 4 + 5 * rows)
    return call(
        kernel,
        name,
        pairs,
        [whole((rows, width))] * 4
        + [
            whole((1, width)),
            columns(rows, 6 * HD),
            columns(rows, 2 * HD),
            per_pair(rows),
            columns(width, 6 * HD),
            lines(2 * HD, width),
            whole((rows, 1)),
            whole((1, rows)),
            whole((rows, width)),
        ],
        [
            (out((rows, width), F32), whole((rows, width))),
            (out((rows, width), BF16), whole((rows, width))),
            (out((1, width), F32), whole((1, width))),
            (out(qkv.shape, BF16), columns(rows, 6 * HD)),
            (out((rows, width), BF16), whole((rows, width))),
            (out((1, width), F32), whole((1, width))),
        ],
        [pltpu.VMEM((rows, width), F32)],
        (
            upper,
            *grads,
            mid,
            gain.reshape(1, width),
            qkv,
            att,
            lse,
            proj,
            mix,
            ids.reshape(rows, 1),
            ids.reshape(1, rows),
            rows_in,
        ),
        flops,
    )


def feed_back(pieces, slope, up, down):
    rows, width = pieces[0].shape
    hidden = up.shape[1]
    block = 256
    steps = hidden // block
    count = len(pieces)

    def kernel(*refs):
        parts = refs[:count]
        sl, u, d, gsum, glow, dpre, dpart, dacc = refs[count:]
        step = pl.program_id(0)

        @pl.when(step == 0)
        def _():
            def body(at):
                value = total(parts, at)
                gsum[at] = value
                glow[at] = value.astype(BF16)

            over_rows(rows, body)

        grad_pre = (mm(glow[...], d[...], 1, 1) * sl[...].astype(F32)).astype(BF16)
        dpre[...] = grad_pre
        share = mm(grad_pre, u[...], 1, 1)

        @pl.when(step == 0)
        def _():
            dacc[...] = share

        @pl.when((step > 0) & (step < steps - 1))
        def _():
            dacc[...] += share

        @pl.when(step == steps - 1)
        def _():
            dpart[...] = (dacc[...] + share).astype(BF16)

    return call(
        kernel,
        "image_feed_back",
        steps,
        [whole((rows, width))] * count
        + [columns(rows, block), columns(width, block), lines(block, width)],
        [
            (out((rows, width), F32), whole((rows, width))),
            (out((rows, width), BF16), whole((rows, width))),
            (out((rows, hidden), BF16), columns(rows, block)),
            (out((rows, width), BF16), whole((rows, width))),
        ],
        [pltpu.VMEM((rows, width), F32)],
        (*pieces, slope, up, down),
        4 * rows * width * hidden,
    )


def local(
    patches,
    captions,
    patch_image,
    caption_image,
    image_norm,
    image_ffnorm,
    text_norm,
    cross_norm,
    text_ffnorm,
    image_proj,
    image_mix,
    image_up,
    image_down,
    text_proj,
    text_mix,
    cross_query,
    cross_keyval,
    cross_mix,
    text_up,
    text_down,
    image_cotan,
    text_cotan,
):
    side = lax.axis_index("mp")
    place = lax.axis_index("dp")
    ring = lax.axis_size("dp")
    image_own = patches.shape[0]
    text_own = captions.shape[0]
    text_rows = 2 * text_own

    def swap(rows):
        return lax.ppermute(rows, "mp", [(0, 1), (1, 0)])

    def both(own_rows):
        other = swap(own_rows)
        return jnp.where(
            side == 0,
            jnp.concatenate((own_rows, other), axis=0),
            jnp.concatenate((other, own_rows), axis=0),
        )

    def own_half(rows, own):
        return lax.dynamic_slice_in_dim(rows, side * own, own)

    def partner(bit):
        return [(i, i ^ (1 << bit)) for i in range(ring)]

    levels = [bit for bit in range(4) if 2 << bit <= ring]

    def reduce_pairs(rows):
        for bit in levels:
            half = rows.shape[0] // 2
            mine = (place >> bit) & 1
            got = lax.ppermute(
                lax.dynamic_slice_in_dim(rows, (1 - mine) * half, half), "dp", partner(bit)
            )
            keep = lax.dynamic_slice_in_dim(rows, mine * half, half)
            rows = (keep.astype(F32) + got.astype(F32)).astype(BF16)
        if ring > 1 << len(levels):
            size = 1 << len(levels)
            groups = [list(range(first, ring, size)) for first in range(size)]
            rows = lax.psum(rows, "dp", axis_index_groups=groups)
        for bit in reversed(levels):
            mine = (place >> bit) & 1
            got = lax.ppermute(rows, "dp", partner(bit))
            rows = jnp.where(
                mine == 0,
                jnp.concatenate((rows, got), axis=0),
                jnp.concatenate((got, rows), axis=0),
            )
        return rows.astype(F32)

    def reduce_all(value):
        value = value + swap(value)
        bit = 0
        while 1 << bit < ring:
            value = value + lax.ppermute(value, "dp", partner(bit))
            bit += 1
        return value

    def weight_grad(left, right):
        return mm(left, right, 0, 0).astype(BF16)

    def stacked(*pieces):
        width = patches.shape[1]
        flat = []
        for piece in pieces:
            if piece.shape[1] < width:
                cut = piece.shape[0] * piece.shape[1] // width
                flat.append(jnp.concatenate((piece[:cut], piece[cut:]), axis=1))
            elif piece.shape[1] % width:
                body = piece.shape[1] // width * width
                flat += [piece[:, i : i + width] for i in range(0, body, width)]
                rest = piece[:, body:]
                cut = rest.shape[0] * rest.shape[1] // width
                flat.append(jnp.concatenate((rest[:cut], rest[cut:]), axis=1))
            else:
                flat += [piece[:, i : i + width] for i in range(0, piece.shape[1], width)]
        return jnp.concatenate(flat, axis=0)

    def unstacked(rows, shapes):
        width = patches.shape[1]
        found, at = [], 0

        def take(count):
            nonlocal at
            at += count
            return rows[at - count : at]

        for height, across in shapes:
            parts = [take(height) for _ in range(across // width)]
            rest = across % width
            if rest:
                cut = take(height * rest // width)
                parts.append(jnp.concatenate((cut[:, :rest], cut[:, rest:]), axis=0))
            found.append(parts[0] if len(parts) == 1 else jnp.concatenate(parts, axis=1))
        return found

    def reduce_stage(*pieces):
        return unstacked(reduce_pairs(stacked(*pieces)), [piece.shape for piece in pieces])

    caption_of = jnp.arange(text_rows, dtype=jnp.int32) // LT
    row_image = jnp.broadcast_to(caption_image[:, None], (caption_image.shape[0], LT))
    row_image = row_image.reshape(text_rows)

    patch_all = both(patches)
    caption_all = both(captions)
    text_cotan_all = both(text_cotan)
    image_cotan_all = both(image_cotan)

    normed_one, image_qkv, image_att, image_lse, mix_part = self_forward(
        patch_all, image_norm, image_proj, image_mix, patch_image, False, "image_self"
    )
    mix_got = swap(mix_part)
    normed_three, text_qkv, text_att, text_lse, text_part = self_forward(
        caption_all, text_norm, text_proj, text_mix, caption_of, True, "text_self"
    )
    text_got = swap(text_part)
    image_mid, normed_two, image_hidden, image_slope, down_part = feed_forward(
        (patch_all, mix_part, mix_got), image_ffnorm, image_up, image_down, "image_feed"
    )
    down_got = swap(down_part)
    (
        embed_all,
        text_mid,
        normed_four,
        cross_q,
        cross_kv,
        cross_att,
        cross_lse,
        cross_part,
    ) = cross_forward(
        (image_mid, down_part, down_got),
        (caption_all, text_part, text_got),
        cross_norm,
        cross_query,
        cross_keyval,
        cross_mix,
        patch_image,
        row_image,
    )
    cross_got = swap(cross_part)
    text_mid2, normed_five, text_hidden, text_dpre, text_down_part, text_dpart = feed_both(
        (text_mid, cross_part, cross_got), text_cotan_all, text_ffnorm, text_up, text_down
    )
    text_dgot = swap(text_dpart)
    text_low = swap(
        lax.dynamic_slice_in_dim(text_down_part, (1 - side) * text_own, text_own)
    )
    text_embed = (
        own_half(text_mid2, text_own)
        + own_half(text_down_part, text_own).astype(F32)
        + text_low.astype(F32)
    ).astype(BF16)
    text_up_grad = weight_grad(normed_five, text_dpre)
    text_down_grad = weight_grad(text_hidden, text_cotan_all)

    (
        grad_mid2,
        grad_mid2_low,
        gain_five,
        dcross_q,
        dcross_kv,
        cross_dpart,
        embed_dpart,
    ) = cross_back(
        text_cotan_all,
        (text_dpart, text_dgot),
        text_mid2,
        text_ffnorm,
        cross_q,
        cross_kv,
        cross_att,
        cross_lse,
        cross_query,
        cross_keyval,
        cross_mix,
        patch_image,
        row_image,
    )
    embed_dgot = swap(embed_dpart)
    cross_dgot = swap(cross_dpart)
    grad_resid, grad_resid_low, image_dpre, feed_dpart = feed_back(
        (image_cotan_all, embed_dpart, embed_dgot), image_slope, image_up, image_down
    )
    feed_dgot = swap(feed_dpart)
    grad_mid, grad_mid_low, gain_four, dtext_qkv, text_dlast, gain_three = self_back(
        grad_mid2,
        (cross_dpart, cross_dgot),
        text_mid,
        cross_norm,
        text_qkv,
        text_att,
        text_lse,
        text_proj,
        text_mix,
        caption_of,
        True,
        caption_all,
        "text_self_back",
    )
    image_up_grad = weight_grad(normed_two, image_dpre)
    image_down_grad = weight_grad(image_hidden, grad_resid_low)
    (
        grad_image_mid,
        grad_image_low,
        gain_two,
        dimage_qkv,
        image_dlast,
        gain_one,
    ) = self_back(
        grad_resid,
        (feed_dpart, feed_dgot),
        image_mid,
        image_ffnorm,
        image_qkv,
        image_att,
        image_lse,
        image_proj,
        image_mix,
        patch_image,
        False,
        patch_all,
        "image_self_back",
    )

    def input_grad(grad_rows, partial_rows, rows_in, gain, own):
        got = swap(lax.dynamic_slice_in_dim(partial_rows, (1 - side) * own, own))
        grad = own_half(partial_rows, own).astype(F32) + got.astype(F32)
        scaled, inv_std = norm_parts(rows_in.astype(F32))
        back = norm_back(grad, scaled, inv_std, gain)
        return (own_half(grad_rows, own) + back).astype(BF16)

    grad_patches = input_grad(grad_image_mid, image_dlast, patches, image_norm, image_own)
    grad_captions = input_grad(grad_mid, text_dlast, captions, text_norm, text_own)

    text_up_sum, text_down_sum = reduce_stage(text_up_grad, text_down_grad)
    mid_sums = reduce_stage(
        weight_grad(normed_three, dtext_qkv),
        weight_grad(text_att, grad_mid_low),
        weight_grad(normed_four, dcross_q),
        weight_grad(embed_all, dcross_kv),
        weight_grad(cross_att, grad_mid2_low),
    )
    image_up_sum, image_down_sum = reduce_stage(image_up_grad, image_down_grad)
    image_proj_sum, image_mix_sum = reduce_stage(
        weight_grad(normed_one, dimage_qkv), weight_grad(image_att, grad_image_low)
    )
    gains = reduce_all(
        jnp.concatenate(
            (gain_one, 0.5 * gain_two, gain_three, 0.5 * gain_four, 0.5 * gain_five), axis=0
        )
    )
    return (
        own_half(embed_all, image_own),
        text_embed,
        grad_patches,
        grad_captions,
        gains[0],
        gains[1],
        gains[2],
        gains[3],
        gains[4],
        image_proj_sum,
        image_mix_sum,
        image_up_sum,
        image_down_sum,
        *mid_sums,
        text_up_sum,
        text_down_sum,
    )


def solution(mesh):
    return jax.shard_map(
        local,
        mesh=mesh,
        in_specs=(
            P(("dp", "mp"), None),
            P(("dp", "mp"), None),
            P("dp"),
            P("dp"),
            P(),
            P(),
            P(),
            P(),
            P(),
            P(None, "mp"),
            P("mp", None),
            P(None, "mp"),
            P("mp", None),
            P(None, "mp"),
            P("mp", None),
            P(None, "mp"),
            P(None, "mp"),
            P("mp", None),
            P(None, "mp"),
            P("mp", None),
            P(("dp", "mp"), None),
            P(("dp", "mp"), None),
        ),
        out_specs=(
            P(("dp", "mp"), None),
            P(("dp", "mp"), None),
            P(("dp", "mp"), None),
            P(("dp", "mp"), None),
            P(),
            P(),
            P(),
            P(),
            P(),
            P(None, "mp"),
            P("mp", None),
            P(None, "mp"),
            P("mp", None),
            P(None, "mp"),
            P("mp", None),
            P(None, "mp"),
            P(None, "mp"),
            P("mp", None),
            P(None, "mp"),
            P("mp", None),
        ),
        check_vma=False,
    )
```

time: 1330 us -> 559 us (0.42)
  waiting for transfers between devices: 734 us -> 248 us
  matrix products: 279 us -> 20.6 us
  Pallas kernels: 0 us -> 129 us
  blocking collectives: 117 us -> 0 us
  local copies, waits for them, and re-layouts: 113 us -> 40.8 us
  starting transfers between devices: 0.96 us -> 60.5 us
    psum x1 -> x0, waiting for transfers between devices: 489 us -> none  [local(): lax.psum((grad_image_proj, grad_image_mix, grad_image_up, grad_image_down...]
    dot_general x159 -> x11, matrix products: 279 us -> 20.6 us  [mm(): lax.dot_general(left, right, (((left_dim,), (right_dim,)), ((), ())), pre...]
    ppermute x0 -> x52, waiting for transfers between devices: none -> 248 us  [the longest x16 104 us: swap(): return lax.ppermute(rows, 'mp', [(0, 1), (1, 0)])]
    reduce_scatter x11 -> x0, waiting for transfers between devices: 181 us -> none  [the longest x5 98.5 us: collect(): return lax.psum_scatter(partial_rows, 'mp', scatter_dimension=0, tiled=True)]
    pallas_call x0 -> x9, Pallas kernels: none -> 129 us  [call(): pl.pallas_call(kernel, name=name, grid=(steps,), in_specs=ins, out_specs=...]
    psum x2 -> x0, blocking collectives: 71.3 us -> none  [the longest x1 64.3 us: local(): lax.psum((grad_image_proj, grad_image_mix, grad_image_up, grad_image_down...]
    all_gather x5 -> x0, waiting for transfers between devices: 64.6 us -> none  [the longest x3 43.9 us: spread(): return lax.all_gather(own_rows, 'mp', axis=0, tiled=True)]
    ppermute x0 -> x52, starting transfers between devices: none -> 60.5 us  [the longest x16 20.1 us: swap(): return lax.ppermute(rows, 'mp', [(0, 1), (1, 0)])]
  transfers between devices with their start and end apart: 17 -> 52, of which waited for: 14 -> 25; matrix products, arithmetic and copies ran while one was open for 15% -> 16% of each run, Pallas kernels for 0% -> 19%
where the time goes in v1:
time: 559 us; the launch traced here: 550 us
  waiting for transfers between devices  248 us (44%)
  Pallas kernels  129 us (23%)
  starting transfers between devices  60.5 us (11%)
  other arithmetic  48.2 us (9%)
  local copies, waits for them, and re-layouts  40.8 us (7%)
  matrix products  20.6 us (4%)
    pallas_call x9, Pallas kernels, call(): pl.pallas_call(kernel, name=name, grid=(steps,), in_specs=ins, out_specs=...  129 us
    ppermute x16, waiting for transfers between devices, swap(): return lax.ppermute(rows, 'mp', [(0, 1), (1, 0)])  104 us
    ppermute x16, waiting for transfers between devices, reduce_pairs(): lax.ppermute(lax.dynamic_slice_in_dim(rows, (1 - mine) * half, half), 'dp...  88.1 us
    ppermute x16, waiting for transfers between devices, reduce_pairs(): got = lax.ppermute(rows, 'dp', partner(bit))  56.2 us
    dot_general x11, matrix products, mm(): lax.dot_general(left, right, (((left_dim,), (right_dim,)), ((), ())), pre...  20.6 us
    ppermute x16, starting transfers between devices, swap(): return lax.ppermute(rows, 'mp', [(0, 1), (1, 0)])  20.1 us
    ppermute x16, starting transfers between devices, reduce_pairs(): got = lax.ppermute(rows, 'dp', partner(bit))  18.3 us
    ppermute x16, starting transfers between devices, reduce_pairs(): lax.ppermute(lax.dynamic_slice_in_dim(rows, (1 - mine) * half, half), 'dp...  17.7 us
  transfers between devices with their start and end apart: 52, of which 25 were waited for; matrix products, arithmetic and copies ran while one was open for 16% of the time, Pallas kernels for 19%

profile of v1, /device:TPU:0, one launch (start us, length us, event | category | flops | bytes accessed | tf_op | source)
XLA Modules:
  0.0 550.1 jit_solution(3663880540659464952)
XLA Ops:
  7.9 9.7 %collective-permute-done = bf16[392,768]{1,0:T(8,128)(2,1)S(1)} collective-permute-done((bf16[392,768]{1,0:T(8,128)(2,1)}, bf16[392,768]{1,0:T(8,128)(2,1)S(1)}, u32[]{:S(2)}, u32[]{:S(2)}) %collective-permute-start) | collective-permute-done | bytes 602144 | tf_op jit(solution)/shard_map/ppermute | solution.py:693
  20.2 16.4 %image_self.1 = (bf16[784,768]{1,0:T(8,128)(2,1)}, bf16[784,1152]{1,0:T(8,128)(2,1)}, bf16[784,384]{1,0:T(8,128)(2,1)}, f32[3,2,784]{2,1,0:T(2,128)}, bf16[784,768]{1,0:T(8,128)(2,1)}) custom-call(bf16[784,768]{1,0:T(8,128)(2,1)} %maximum_select_fusion.7.x.refs_0_, f32[1,768]{1,0:T(1,128)} %reshape.183.g, bf16[768,1152]{1,0:T(8,128)(2,1)} %w.6, ...), custom_call_target="tpu_custom_call" | custom-call | flops 2793799680 | bytes 8408576 | tf_op jit(solution)/shard_map/image_self/pallas_call | solution.py:156
  42.3 24.0 %collective-permute-done.1.refs_2_ = bf16[784,768]{1,0:T(8,128)(2,1)S(1)} collective-permute-done((bf16[784,768]{1,0:T(8,128)(2,1)}, bf16[784,768]{1,0:T(8,128)(2,1)S(1)}, u32[]{:S(2)}, u32[]{:S(2)}) %collective-permute-start.1) | collective-permute-done | bytes 1204256 | tf_op jit(solution)/shard_map/ppermute | solution.py:693
  67.3 16.8 %image_feed.1 = (f32[784,768]{1,0:T(8,128)}, bf16[784,768]{1,0:T(8,128)(2,1)}, bf16[784,1536]{1,0:T(8,128)(2,1)}, bf16[784,1536]{1,0:T(8,128)(2,1)}, bf16[784,768]{1,0:T(8,128)(2,1)}) custom-call(bf16[784,768]{1,0:T(8,128)(2,1)} %maximum_select_fusion.7.x.refs_0_, bf16[784,768]{1,0:T(8,128)(2,1)} %get-tuple-element.72.refs_1_, bf16[784,768]{1,0:T(8,128)(2,1)} %copy-done.45, ...), custom_call_target="tpu_custom_call" | custom-call | flops 3699376128 | bytes 17968128 | tf_op jit(solution)/shard_map/image_feed/pallas_call | solution.py:156
  88.8 7.0 %text_self.1 = (bf16[256,768]{1,0:T(8,128)(2,1)}, bf16[256,1152]{1,0:T(8,128)(2,1)}, bf16[256,384]{1,0:T(8,128)(2,1)}, f32[3,2,256]{2,1,0:T(2,128)}, bf16[256,768]{1,0:T(8,128)(2,1)}) custom-call(bf16[256,768]{1,0:T(8,128)(2,1)} %maximum_select_fusion.17.x.refs_3_, f32[1,768]{1,0:T(1,128)} %reshape.187.g, bf16[768,1152]{1,0:T(8,128)(2,1)} %w.7, ...), custom_call_target="tpu_custom_call" | custom-call | flops 704643072 | bytes 4336640 | tf_op jit(solution)/shard_map/text_self/pallas_call | solution.py:156
  97.0 23.1 %collective-permute-done.4.refs_5_ = bf16[256,768]{1,0:T(8,128)(2,1)S(1)} collective-permute-done((bf16[256,768]{1,0:T(8,128)(2,1)}, bf16[256,768]{1,0:T(8,128)(2,1)S(1)}, u32[]{:S(2)}, u32[]{:S(2)}) %collective-permute-start.4) | collective-permute-done | bytes 393248 | tf_op jit(solution)/shard_map/ppermute | solution.py:693
  121.3 12.9 %cross_forward.1 = (bf16[784,768]{1,0:T(8,128)(2,1)}, f32[256,768]{1,0:T(8,128)}, bf16[256,768]{1,0:T(8,128)(2,1)}, bf16[256,384]{1,0:T(8,128)(2,1)}, bf16[784,7...) custom-call(f32[784,768]{1,0:T(8,128)} %get-tuple-element.73.refs_0_.md, ...), custom_call_target="tpu_custom_call" | custom-call | flops 1535115264 | bytes 12743744 | tf_op jit(solution)/shard_map/cross_forward/pallas_call | solution.py:156
  144.3 9.9 %text_feed.1 = (f32[256,768]{1,0:T(8,128)}, bf16[256,768]{1,0:T(8,128)(2,1)}, bf16[256,1536]{1,0:T(8,128)(2,1)}, bf16[256,1536]{1,0:T(8,128)(2,1)}, bf16[256,768]{1,0:T(8,128)(2,1)}, /*index=5*/bf16[256,768]{1,0:T(8,128)(2,1)}) custom-call(f32[256,768]{1,0:T(8,128)} %get-tuple-element.77.refs_0_.md, bf16[256,768]{1,0:T(8,128)(2,1)} %get-tuple-element.78.refs_1_, ...), custom_call_target="tpu_custom_call" | custom-call | flops 2415919104 | bytes 10226688 | tf_op jit(solution)/shard_map/text_feed/pallas_call | solution.py:156
  168.6 12.2 %cross_back.1 = (f32[256,768]{1,0:T(8,128)}, bf16[256,768]{1,0:T(8,128)(2,1)}, f32[1,768]{1,0:T(1,128)}, bf16[256,384]{1,0:T(8,128)(2,1)}, bf16[784,768]{1,0:T(8...) custom-call(bf16[256,768]{1,0:T(8,128)(2,1)} %maximum_select_fusion.18.refs_3_.up0, ...), custom_call_target="tpu_custom_call" | custom-call | flops 1997537280 | bytes 10117184 | tf_op jit(solution)/shard_map/cross_back/pallas_call | solution.py:156
  185.5 28.7 %collective-permute-done.13.g1 = bf16[256,768]{1,0:T(8,128)(2,1)S(1)} collective-permute-done((bf16[256,768]{1,0:T(8,128)(2,1)}, bf16[256,768]{1,0:T(8,128)(2,1)S(1)}, u32[]{:S(2)}, u32[]{:S(2)}) %collective-permute-start.13) | collective-permute-done | bytes 393248 | tf_op jit(solution)/shard_map/ppermute | solution.py:693
  215.0 10.2 %text_self_back.1 = (f32[256,768]{1,0:T(8,128)}, bf16[256,768]{1,0:T(8,128)(2,1)}, f32[1,768]{1,0:T(1,128)}, bf16[256,1152]{1,0:T(8,128)(2,1)}, bf16[256,768]{1,0:T(8,128)(2,1)}, /*index=5*/f32[1,768]{1,0:T(1,128)}) custom-call(f32[256,768]{1,0:T(8,128)} %get-tuple-element.95.up0, bf16[256,768]{1,0:T(8,128)(2,1)} %get-tuple-element.96.g0, ...), custom_call_target="tpu_custom_call" | custom-call | flops 855638016 | bytes 8078336 | tf_op jit(solution)/shard_map/text_self_back/pallas_call | solution.py:156
  236.5 15.0 %image_feed_back.1 = (f32[784,768]{1,0:T(8,128)}, bf16[784,768]{1,0:T(8,128)(2,1)}, bf16[784,1536]{1,0:T(8,128)(2,1)}, bf16[784,768]{1,0:T(8,128)(2,1)}) custom-call(bf16[784,768]{1,0:T(8,128)(2,1)} %maximum_select_fusion.8.refs_0_, bf16[784,768]{1,0:T(8,128)(2,1)} %get-tuple-element.86.refs_1_, bf16[784,768]{1,0:T(8,128)(2,1)} %copy-done.44, ...), custom_call_target="tpu_custom_call" | custom-call | flops 3699376128 | bytes 17965056 | tf_op jit(solution)/shard_map/image_feed_back/pallas_call | solution.py:156
  270.2 10.5 %collective-permute-done.11.g1 = bf16[784,768]{1,0:T(8,128)(2,1)} collective-permute-done((bf16[784,768]{1,0:T(8,128)(2,1)}, bf16[784,768]{1,0:T(8,128)(2,1)}, u32[]{:S(2)}, u32[]{:S(2)}) %collective-permute-start.11) | collective-permute-done | bytes 1204256 | tf_op jit(solution)/shard_map/ppermute | solution.py:693
  280.8 29.0 %image_self_back.1 = (f32[784,768]{1,0:T(8,128)}, bf16[784,768]{1,0:T(8,128)(2,1)}, f32[1,768]{1,0:T(1,128)}, bf16[784,1152]{1,0:T(8,128)(2,1)}, bf16[784,768]{1,0:T(8,128)(2,1)}, /*index=5*/f32[1,768]{1,0:T(1,128)}) custom-call(f32[784,768]{1,0:T(8,128)} %get-tuple-element.88.up0, bf16[784,768]{1,0:T(8,128)(2,1)} %get-tuple-element.89.g0, ...), custom_call_target="tpu_custom_call" | custom-call | flops 4209967104 | bytes 19854848 | tf_op jit(solution)/shard_map/image_self_back/pallas_call | solution.py:156
  334.2 9.0 %collective-permute-done.46 = bf16[384,768]{1,0:T(8,128)(2,1)S(1)} collective-permute-done((bf16[384,768]{1,0:T(8,128)(2,1)S(1)}, bf16[384,768]{1,0:T(8,128)(2,1)S(1)}, u32[]{:S(2)}, u32[]{:S(2)}) %collective-permute-start.46) | collective-permute-done | bytes 589856 | tf_op jit(solution)/shard_map/ppermute | solution.py:715
  345.5 8.7 %collective-permute-done.37 = bf16[768,768]{1,0:T(8,128)(2,1)S(1)} collective-permute-done((bf16[768,768]{1,0:T(8,128)(2,1)S(1)}, bf16[768,768]{1,0:T(8,128)(2,1)S(1)}, u32[]{:S(2)}, u32[]{:S(2)}) %collective-permute-start.37) | collective-permute-done | bytes 1179680 | tf_op jit(solution)/shard_map/ppermute | solution.py:715
  359.0 32.1 %collective-permute-done.21 = bf16[384,768]{1,0:T(8,128)(2,1)S(1)} collective-permute-done((bf16[384,768]{1,0:T(8,128)(2,1)S(1)}, bf16[384,768]{1,0:T(8,128)(2,1)S(1)}, u32[]{:S(2)}, u32[]{:S(2)}) %collective-permute-start.21) | collective-permute-done | bytes 589856 | tf_op jit(solution)/shard_map/ppermute | solution.py:715
  404.7 11.9 %collective-permute-done.23 = bf16[96,768]{1,0:T(8,128)(2,1)S(1)} collective-permute-done((bf16[96,768]{1,0:T(8,128)(2,1)S(1)}, bf16[96,768]{1,0:T(8,128)(2,1)S(1)}, u32[]{:S(2)}, u32[]{:S(2)}) %collective-permute-start.23) | collective-permute-done | bytes 147488 | tf_op jit(solution)/shard_map/ppermute | solution.py:715
  436.2 10.8 %collective-permute-done.30 = bf16[384,768]{1,0:T(8,128)(2,1)S(1)} collective-permute-done((bf16[384,768]{1,0:T(8,128)(2,1)S(1)}, bf16[384,768]{1,0:T(8,128)(2,1)S(1)}, u32[]{:S(2)}, u32[]{:S(2)}) %collective-permute-start.30) | collective-permute-done | bytes 589856 | tf_op jit(solution)/shard_map/ppermute | solution.py:715
  457.4 7.2 %collective-permute-done.31 = bf16[192,768]{1,0:T(8,128)(2,1)S(1)} collective-permute-done((bf16[192,768]{1,0:T(8,128)(2,1)S(1)}, bf16[192,768]{1,0:T(8,128)(2,1)S(1)}, u32[]{:S(2)}, u32[]{:S(2)}) %collective-permute-start.31) | collective-permute-done | bytes 294944 | tf_op jit(solution)/shard_map/ppermute | solution.py:715
  465.4 7.7 %collective-permute-done.26 = bf16[384,768]{1,0:T(8,128)(2,1)S(1)} collective-permute-done((bf16[384,768]{1,0:T(8,128)(2,1)S(1)}, bf16[384,768]{1,0:T(8,128)(2,1)S(1)}, u32[]{:S(2)}, u32[]{:S(2)}) %collective-permute-start.26) | collective-permute-done | bytes 589856 | tf_op jit(solution)/shard_map/ppermute | solution.py:726
  483.4 9.1 %collective-permute-done.33 = bf16[384,768]{1,0:T(8,128)(2,1)S(1)} collective-permute-done((bf16[384,768]{1,0:T(8,128)(2,1)S(1)}, bf16[384,768]{1,0:T(8,128)(2,1)S(1)}, u32[]{:S(2)}, u32[]{:S(2)}) %collective-permute-start.33) | collective-permute-done | bytes 589856 | tf_op jit(solution)/shard_map/ppermute | solution.py:726
  495.9 10.1 %collective-permute-done.42 = bf16[768,768]{1,0:T(8,128)(2,1)S(1)} collective-permute-done((bf16[768,768]{1,0:T(8,128)(2,1)S(1)}, bf16[768,768]{1,0:T(8,128)(2,1)S(1)}, u32[]{:S(2)}, u32[]{:S(2)}) %collective-permute-start.42) | collective-permute-done | bytes 1179680 | tf_op jit(solution)/shard_map/ppermute | solution.py:726
  510.6 17.2 %collective-permute-done.34 = bf16[768,768]{1,0:T(8,128)(2,1)S(1)} collective-permute-done((bf16[768,768]{1,0:T(8,128)(2,1)S(1)}, bf16[768,768]{1,0:T(8,128)(2,1)S(1)}, u32[]{:S(2)}, u32[]{:S(2)}) %collective-permute-start.34) | collective-permute-done | bytes 1179680 | tf_op jit(solution)/shard_map/ppermute | solution.py:726
  (336 shorter events, 198.5 us)
Async XLA Ops:
  36.6 29.6 %collective-permute-start.1 = (bf16[784,768]{1,0:T(8,128)(2,1)}, bf16[784,768]{1,0:T(8,128)(2,1)S(1)}, u32[]{:S(2)}, u32[]{:S(2)}) collective-permute-start(bf16[784,768]{1,0:T(8,128)(2,1)} %get-tuple-element.72.refs_1_), channel_id=1, source_target_pairs={{0,1},{1,0},{2,3},{3,2},{4,5},{5,4},{6,7},{7,6},{8,9},{9,8},{10,11... | collective-permute-start | bytes 3612680 | tf_op jit(solution)/shard_map/ppermute | solution.py:693
  38.4 49.5 %collective-permute-start.3 = (bf16[128,768]{1,0:T(8,128)(2,1)S(1)}, bf16[128,768]{1,0:T(8,128)(2,1)S(1)}, u32[]{:S(2)}, u32[]{:S(2)}) collective-permute-start(bf16[128,768]{1,0:T(8,128)(2,1)S(1)} %copy-done.3), channel_id=1, source_target_pairs={{0,1},{1,0},{2,3},{3,2},{4,5},{5,4},{6,7},{7,6},{8,9},{9,8},{10,11... | collective-permute-start | bytes 589832 | tf_op jit(solution)/shard_map/ppermute | solution.py:693
  38.7 97.5 %collective-permute-start.6 = (bf16[128,768]{1,0:T(8,128)(2,1)S(1)}, bf16[128,768]{1,0:T(8,128)(2,1)S(1)}, u32[]{:S(2)}, u32[]{:S(2)}) collective-permute-start(bf16[128,768]{1,0:T(8,128)(2,1)S(1)} %copy-done.27), channel_id=1, source_target_pairs={{0,1},{1,0},{2,3},{3,2},{4,5},{5,4},{6,7},{7,6},{8,9},{9,8},{10,11... | collective-permute-start | bytes 589832 | tf_op jit(solution)/shard_map/ppermute | solution.py:693
  40.5 96.6 %collective-permute-start.8 = (bf16[392,768]{1,0:T(8,128)(2,1)S(1)}, bf16[392,768]{1,0:T(8,128)(2,1)}, u32[]{:S(2)}, u32[]{:S(2)}) collective-permute-start(bf16[392,768]{1,0:T(8,128)(2,1)S(1)} %copy-done.13), channel_id=1, source_target_pairs={{0,1},{1,0},{2,3},{3,2},{4,5},{5,4},{6,7},{7,6},{8,9},{9,8},{10,11... | collective-permute-start | bytes 1806344 | tf_op jit(solution)/shard_map/ppermute | solution.py:693
  84.1 36.0 %collective-permute-start.2 = (bf16[784,768]{1,0:T(8,128)(2,1)}, bf16[784,768]{1,0:T(8,128)(2,1)S(1)}, u32[]{:S(2)}, u32[]{:S(2)}) collective-permute-start(bf16[784,768]{1,0:T(8,128)(2,1)} %get-tuple-element.74.refs_1_), channel_id=1, source_target_pairs={{0,1},{1,0},{2,3},{3,2},{4,5},{5,4},{6,7},{7,6},{8,9},{9,8},{10,11... | collective-permute-start | bytes 3612680 | tf_op jit(solution)/shard_map/ppermute | solution.py:693
  162.4 103.8 %collective-permute-start.44 = (bf16[1536,768]{1,0:T(8,128)(2,1)}, bf16[1536,768]{1,0:T(8,128)(2,1)}, u32[]{:S(2)}, u32[]{:S(2)}) collective-permute-start(bf16[1536,768]{1,0:T(8,128)(2,1)} %constant_dynamic-slice_fusion.3), channel_id=1, source_target_pairs={{0,2},{2,0},{4,6},{6,4},{8,10},{10,8},{12,14},{14,12},{16,18},{18,... | collective-permute-start | bytes 7077896 | tf_op jit(solution)/shard_map/ppermute | solution.py:715
  180.8 54.6 %collective-permute-start.10 = (bf16[784,768]{1,0:T(8,128)(2,1)}, bf16[784,768]{1,0:T(8,128)(2,1)S(1)}, u32[]{:S(2)}, u32[]{:S(2)}) collective-permute-start(bf16[784,768]{1,0:T(8,128)(2,1)} %get-tuple-element.86.refs_1_), channel_id=1, source_target_pairs={{0,1},{1,0},{2,3},{3,2},{4,5},{5,4},{6,7},{7,6},{8,9},{9,8},{10,11... | collective-permute-start | bytes 3612680 | tf_op jit(solution)/shard_map/ppermute | solution.py:693
  181.7 32.5 %collective-permute-start.13 = (bf16[256,768]{1,0:T(8,128)(2,1)}, bf16[256,768]{1,0:T(8,128)(2,1)S(1)}, u32[]{:S(2)}, u32[]{:S(2)}) collective-permute-start(bf16[256,768]{1,0:T(8,128)(2,1)} %get-tuple-element.96.g0), channel_id=1, source_target_pairs={{0,1},{1,0},{2,3},{3,2},{4,5},{5,4},{6,7},{7,6},{8,9},{9,8},{10,11... | collective-permute-start | bytes 1179656 | tf_op jit(solution)/shard_map/ppermute | solution.py:693
  234.0 88.8 %collective-permute-start.36 = (bf16[1536,768]{1,0:T(8,128)(2,1)}, bf16[1536,768]{1,0:T(8,128)(2,1)}, u32[]{:S(2)}, u32[]{:S(2)}) collective-permute-start(bf16[1536,768]{1,0:T(8,128)(2,1)} %constant_dynamic-slice_fusion.7), channel_id=1, source_target_pairs={{0,2},{2,0},{4,6},{6,4},{8,10},{10,8},{12,14},{14,12},{16,18},{18,... | collective-permute-start | bytes 7077896 | tf_op jit(solution)/shard_map/ppermute | solution.py:715
  251.5 29.3 %collective-permute-start.11 = (bf16[784,768]{1,0:T(8,128)(2,1)}, bf16[784,768]{1,0:T(8,128)(2,1)}, u32[]{:S(2)}, u32[]{:S(2)}) collective-permute-start(bf16[784,768]{1,0:T(8,128)(2,1)} %get-tuple-element.89.g0), channel_id=1, source_target_pairs={{0,1},{1,0},{2,3},{3,2},{4,5},{5,4},{6,7},{7,6},{8,9},{9,8},{10,11... | collective-permute-start | bytes 3612680 | tf_op jit(solution)/shard_map/ppermute | solution.py:693
  266.0 63.2 %collective-permute-start.28 = (bf16[1536,768]{1,0:T(8,128)(2,1)}, bf16[1536,768]{1,0:T(8,128)(2,1)}, u32[]{:S(2)}, u32[]{:S(2)}) collective-permute-start(bf16[1536,768]{1,0:T(8,128)(2,1)} %constant_dynamic-slice_fusion.11), channel_id=1, source_target_pairs={{0,2},{2,0},{4,6},{6,4},{8,10},{10,8},{12,14},{14,12},{16,18},{18,... | collective-permute-start | bytes 7077896 | tf_op jit(solution)/shard_map/ppermute | solution.py:715
  269.5 57.2 %collective-permute-start.45 = (bf16[768,768]{1,0:T(8,128)(2,1)}, bf16[768,768]{1,0:T(8,128)(2,1)}, u32[]{:S(2)}, u32[]{:S(2)}) collective-permute-start(bf16[768,768]{1,0:T(8,128)(2,1)} %constant_dynamic-slice_fusion.2), channel_id=1, source_target_pairs={{0,4},{2,6},{4,0},{6,2},{8,12},{10,14},{12,8},{14,10},{16,20},{18,... | collective-permute-start | bytes 3538952 | tf_op jit(solution)/shard_map/ppermute | solution.py:715
  322.1 70.8 %collective-permute-start.17 = (f32[5,768]{1,0:T(8,128)S(1)}, f32[5,768]{1,0:T(8,128)S(1)}, u32[]{:S(2)}, u32[]{:S(2)}) collective-permute-start(f32[5,768]{1,0:T(8,128)S(1)} %add.215), channel_id=1, source_target_pairs={{0,4},{2,6},{4,0},{6,2},{8,12},{10,14},{12,8},{14,10},{16,20},{18,... | collective-permute-start | bytes 46088 | tf_op jit(solution)/shard_map/ppermute | solution.py:738
  325.3 28.9 %collective-permute-start.37 = (bf16[768,768]{1,0:T(8,128)(2,1)S(1)}, bf16[768,768]{1,0:T(8,128)(2,1)S(1)}, u32[]{:S(2)}, u32[]{:S(2)}) collective-permute-start(bf16[768,768]{1,0:T(8,128)(2,1)S(1)} %constant_dynamic-slice_fusion.6), channel_id=1, source_target_pairs={{0,4},{2,6},{4,0},{6,2},{8,12},{10,14},{12,8},{14,10},{16,20},{18,... | collective-permute-start | bytes 3538952 | tf_op jit(solution)/shard_map/ppermute | solution.py:715
  331.6 88.6 %collective-permute-start.29 = (bf16[768,768]{1,0:T(8,128)(2,1)S(1)}, bf16[768,768]{1,0:T(8,128)(2,1)S(1)}, u32[]{:S(2)}, u32[]{:S(2)}) collective-permute-start(bf16[768,768]{1,0:T(8,128)(2,1)S(1)} %constant_dynamic-slice_fusion.10), channel_id=1, source_target_pairs={{0,4},{2,6},{4,0},{6,2},{8,12},{10,14},{12,8},{14,10},{16,20},{18,... | collective-permute-start | bytes 3538952 | tf_op jit(solution)/shard_map/ppermute | solution.py:715
  333.6 57.6 %collective-permute-start.21 = (bf16[384,768]{1,0:T(8,128)(2,1)S(1)}, bf16[384,768]{1,0:T(8,128)(2,1)S(1)}, u32[]{:S(2)}, u32[]{:S(2)}) collective-permute-start(bf16[384,768]{1,0:T(8,128)(2,1)S(1)} %constant_dynamic-slice_fusion.14), channel_id=1, source_target_pairs={{0,4},{2,6},{4,0},{6,2},{8,12},{10,14},{12,8},{14,10},{16,20},{18,... | collective-permute-start | bytes 1769480 | tf_op jit(solution)/shard_map/ppermute | solution.py:715
  354.6 49.3 %collective-permute-start.38 = (bf16[384,768]{1,0:T(8,128)(2,1)S(1)}, bf16[384,768]{1,0:T(8,128)(2,1)S(1)}, u32[]{:S(2)}, u32[]{:S(2)}) collective-permute-start(bf16[384,768]{1,0:T(8,128)(2,1)S(1)} %constant_dynamic-slice_fusion.5), channel_id=1, source_target_pairs={{0,8},{2,10},{4,12},{6,14},{8,0},{10,2},{12,4},{14,6},{16,24},{18,... | collective-permute-start | bytes 1769480 | tf_op jit(solution)/shard_map/ppermute | solution.py:715
  358.5 35.1 %collective-permute-start.48 = (bf16[192,768]{1,0:T(8,128)(2,1)S(1)}, bf16[192,768]{1,0:T(8,128)(2,1)S(1)}, u32[]{:S(2)}, u32[]{:S(2)}) collective-permute-start(bf16[192,768]{1,0:T(8,128)(2,1)S(1)} %add_convert_fusion.11), channel_id=1, source_target_pairs={{0,16},{2,18},{4,20},{6,22},{8,24},{10,26},{12,28},{14,30},{16,0},... | collective-permute-start | bytes 884744 | tf_op jit(solution)/shard_map/ppermute | solution.py:726
  393.7 41.9 %collective-permute-start.49 = (bf16[384,768]{1,0:T(8,128)(2,1)S(1)}, bf16[384,768]{1,0:T(8,128)(2,1)S(1)}, u32[]{:S(2)}, u32[]{:S(2)}) collective-permute-start(bf16[384,768]{1,0:T(8,128)(2,1)S(1)} %maximum_select_fusion.16), channel_id=1, source_target_pairs={{0,8},{2,10},{4,12},{6,14},{8,0},{10,2},{12,4},{14,6},{16,24},{18,... | collective-permute-start | bytes 1769480 | tf_op jit(solution)/shard_map/ppermute | solution.py:726
  421.7 34.1 %collective-permute-start.19 = (f32[5,768]{1,0:T(8,128)S(1)}, f32[5,768]{1,0:T(8,128)S(1)}, u32[]{:S(2)}, u32[]{:S(2)}) collective-permute-start(f32[5,768]{1,0:T(8,128)S(1)} %add.217), channel_id=1, source_target_pairs={{0,16},{2,18},{4,20},{6,22},{8,24},{10,26},{12,28},{14,30},{16,0},... | collective-permute-start | bytes 46088 | tf_op jit(solution)/shard_map/ppermute | solution.py:738
  436.1 44.3 %collective-permute-start.50 = (bf16[768,768]{1,0:T(8,128)(2,1)S(1)}, bf16[768,768]{1,0:T(8,128)(2,1)S(1)}, u32[]{:S(2)}, u32[]{:S(2)}) collective-permute-start(bf16[768,768]{1,0:T(8,128)(2,1)S(1)} %maximum_select_fusion.12), channel_id=1, source_target_pairs={{0,4},{2,6},{4,0},{6,2},{8,12},{10,14},{12,8},{14,10},{16,20},{18,... | collective-permute-start | bytes 3538952 | tf_op jit(solution)/shard_map/ppermute | solution.py:726
  473.5 33.1 %collective-permute-start.27 = (bf16[768,768]{1,0:T(8,128)(2,1)S(1)}, bf16[768,768]{1,0:T(8,128)(2,1)S(1)}, u32[]{:S(2)}, u32[]{:S(2)}) collective-permute-start(bf16[768,768]{1,0:T(8,128)(2,1)S(1)} %maximum_select_fusion.9), channel_id=1, source_target_pairs={{0,2},{2,0},{4,6},{6,4},{8,10},{10,8},{12,14},{14,12},{16,18},{18,... | collective-permute-start | bytes 3538952 | tf_op jit(solution)/shard_map/ppermute | solution.py:726
  481.1 47.4 %collective-permute-start.51 = (bf16[1536,768]{1,0:T(8,128)(2,1)S(1)}, bf16[1536,768]{1,0:T(8,128)(2,1)S(1)}, u32[]{:S(2)}, u32[]{:S(2)}) collective-permute-start(bf16[1536,768]{1,0:T(8,128)(2,1)S(1)} %maximum_select_fusion.6), channel_id=1, source_target_pairs={{0,2},{2,0},{4,6},{6,4},{8,10},{10,8},{12,14},{14,12},{16,18},{18,... | collective-permute-start | bytes 7077896 | tf_op jit(solution)/shard_map/ppermute | solution.py:726
  492.9 34.9 %collective-permute-start.34 = (bf16[768,768]{1,0:T(8,128)(2,1)S(1)}, bf16[768,768]{1,0:T(8,128)(2,1)S(1)}, u32[]{:S(2)}, u32[]{:S(2)}) collective-permute-start(bf16[768,768]{1,0:T(8,128)(2,1)S(1)} %maximum_select_fusion.10), channel_id=1, source_target_pairs={{0,4},{2,6},{4,0},{6,2},{8,12},{10,14},{12,8},{14,10},{16,20},{18,... | collective-permute-start | bytes 3538952 | tf_op jit(solution)/shard_map/ppermute | solution.py:726
  (86 other events, 1261.5 us)
